TPU v7x, 32 devices: a whole 2x2x4 slice. The times are simulated.
32 devices in a mesh: tm: 8 (over z, y), space: 4 (over x, core).
Axes of the slice: x: 2, y: 2, z: 4, core: 2. Of those that a mesh axis runs over, the one named last changes fastest.
Arguments:
- initial: float32 [8, 128, 128], P('space'), may hold values from -6 to 6
- start_guess: float32 [8, 8, 128, 128], P('tm', 'space'), may hold values from -6 to 6
- forcing: float32 [8, 5, 8, 128, 128], P('tm', None, 'space'), may hold values from -6 to 6
- step_size: float32 [8], P('tm'), may hold values from 0.06 to 0.16
Outputs:
- fine_values: float32 [8, 5, 8, 128, 128], P('tm', None, 'space')
All inputs are finite; a program needn't handle non-finite values.
Results may differ from a plain program's by a relative error of at most 0.0001.
Values sent between devices are 32-bit elements; how exact they have to be, the bound alone decides.
A program may use at most 64 MiB of HBM per device.

v0:
```python
import functools
import math

import jax
import jax.numpy as jnp
import numpy as np
from jax import lax
from jax.experimental import pallas as pl
from jax.experimental.pallas import tpu as pltpu
from jax.sharding import PartitionSpec as P

MESH = pl.DeviceIdType.MESH
CHUNKS = 2


def node_tables():
    radical = math.sqrt(3.0 / 7.0)
    node_times = [0.0, (1.0 - radical) / 2.0, 0.5, (1.0 + radical) / 2.0, 1.0]
    integrals = np.zeros((4, 5))
    for column in range(5):
        coeffs = [1.0]
        for other_index in range(5):
            if other_index == column:
                continue
            other_time = node_times[other_index]
            scaling = node_times[column] - other_time
            grown = [0.0] * (len(coeffs) + 1)
            for exponent in range(len(coeffs)):
                grown[exponent + 1] += coeffs[exponent] / scaling
                grown[exponent] -= coeffs[exponent] * other_time / scaling
            coeffs = grown
        for section in range(4):
            integrals[section, column] = sum(
                (
                    coeffs[exponent]
                    * (
                        node_times[section + 1] ** (exponent + 1)
                        - node_times[section] ** (exponent + 1)
                    )
                    / (exponent + 1)
                    for exponent in range(len(coeffs))
                )
            )
    coarse = [0.0, 0.5, 1.0]
    interp = np.zeros((5, 3))
    for column in range(3):
        for section in range(5):
            weight = 1.0
            for other_index in range(3):
                if other_index != column:
                    weight = (
                        weight
                        * (node_times[section] - coarse[other_index])
                        / (coarse[column] - coarse[other_index])
                    )
            interp[section, column] = weight
    return (np.array(node_times), integrals, interp)


def sine(length):
    k = np.arange(1, length + 1)
    phase = np.outer(k, k) % (2 * (length + 1))
    return math.sqrt(2.0 / (length + 1)) * np.sin(math.pi / (length + 1) * phase)


def eigen(length):
    return 2.0 - 2.0 * np.cos(math.pi / (length + 1) * np.arange(1, length + 1))


def split_pair(value):
    high = value.astype(jnp.bfloat16)
    return high, (value - high.astype(jnp.float32)).astype(jnp.bfloat16)


def dot(a, b):
    return jnp.dot(a, b, preferred_element_type=jnp.float32)


def precise(a, b):
    return dot(a[0], b[0]) + (dot(a[1], b[0]) + dot(a[0], b[1]))


def lateral(field, x_pair, y_pair):
    depth, width_x, width_y = field.shape
    mixed = precise(split_pair(field.reshape(depth * width_x, width_y)), y_pair)
    return [
        precise(x_pair, split_pair(mixed[z * width_x : (z + 1) * width_x])) for z in range(depth)
    ]


def z_sine(planes):
    count = len(planes)
    table = sine(count)
    half = (count + 1) // 2
    pairs = [
        (planes[z] + planes[count - 1 - z], planes[z] - planes[count - 1 - z])
        if z != count - 1 - z
        else (planes[z], None)
        for z in range(half)
    ]
    out = []
    for k in range(count):
        terms = [
            float(table[k, z]) * pairs[z][k % 2] for z in range(half) if pairs[z][k % 2] is not None
        ]
        total = terms[0]
        for term in terms[1:]:
            total = total + term
        out.append(total)
    return out


def weighted(weights, items):
    total = None
    for weight, item in zip(weights, items):
        weight = float(weight)
        if weight == 0.0 or item is None:
            continue
        term = item if weight == 1.0 else weight * item
        total = term if total is None else total + term
    return total


def sweep(rate, nodes, sources):
    times, integrals, _ = TABLES
    swept = [nodes[0]]
    for m in range(4):
        spacing = float(times[m + 1] - times[m])
        inner = weighted(integrals[m], nodes)
        if m > 0:
            inner = inner + spacing * (swept[m] - nodes[m])
        step = rate * inner
        if swept[m] is not None:
            step = step + swept[m]
        if sources is not None:
            step = step + sources[m]
        swept.append(step)
    first = list(integrals[0] + integrals[1])
    second = list(integrals[2] + integrals[3])
    first[0] -= 0.5
    second[2] -= 0.5
    left = rate * weighted(first, swept)
    right = rate * weighted(second, swept)
    if sources is not None:
        left = left + (sources[0] + sources[1])
        right = right + (sources[2] + sources[3])
    return swept, left, right


def corrected(swept, left, right, middle):
    interp = TABLES[2]
    ending = middle * left + right
    deltas = [None if swept[0] is None else -swept[0], left - swept[2], ending - swept[4]]
    return [
        None,
        swept[1] + weighted(interp[1], deltas),
        left,
        swept[3] + weighted(interp[3], deltas),
        ending,
    ]


def start_gains(middle):
    interp = TABLES[2]
    square = middle * middle
    return [
        None,
        float(interp[1, 0]) + float(interp[1, 1]) * middle + float(interp[1, 2]) * square,
        middle,
        float(interp[3, 0]) + float(interp[3, 1]) * middle + float(interp[3, 2]) * square,
        square,
    ]


def gains_of(rate):
    middle = 1.0 + 0.5 * rate
    gains = start_gains(middle)
    nodes = [jnp.ones_like(middle)] + gains[1:]
    swept, left, right = sweep(rate, nodes, None)
    return gains, corrected(swept, left, right, middle)


TABLES = node_tables()


def kernel(
    dims,
    step_ref, initial_hbm, guess_hbm, forcing_hbm, x_hbm, y_hbm, lateral_hbm,
    result_ref,
    initial, guess, forcing, x_ref, y_ref, lateral_ref,
    in_send, in_recv, ghat, hhat, ell, own_step, steps,
    gain_c, gain_d, part_b, z_send, z_recv, own_gain, own_cross, r_send, r_recv,
    o_send, o_recv,
    load_sem, in_ss, in_rs, h_ss, h_rs, s_ss, s_rs, z_ss, z_rs, r_ss, r_rs, o_ss, o_rs,
):
    spaces, slices, chunks, depth, length_z, rows, width_y, owners, block = dims
    me = lax.axis_index("space")
    place = lax.axis_index("tm")
    _, integrals, _ = TABLES
    width_x = spaces * chunks * rows

    barrier = pltpu.get_barrier_semaphore()
    for i in range(1, spaces):
        pl.semaphore_signal(
            barrier, inc=1, device_id={"space": lax.rem(me + i, spaces)}, device_id_type=MESH
        )

    def greet(i, carry):
        pl.semaphore_signal(
            barrier, inc=1, device_id={"tm": lax.rem(place + i, slices)}, device_id_type=MESH
        )
        return carry

    lax.fori_loop(1, slices, greet, 0)

    sources = (guess_hbm.at[0], x_hbm, y_hbm, forcing_hbm.at[0], initial_hbm, lateral_hbm)
    loads = [
        pltpu.make_async_copy(source, target, load_sem.at[i])
        for i, (source, target) in enumerate(
            zip(sources, (guess, x_ref, y_ref, forcing, initial, lateral_ref))
        )
    ]
    for load in loads:
        load.start()
    load_guess, load_x, load_y, load_forcing, load_initial, load_lateral = loads

    step = step_ref[0]
    own_step[...] = jnp.full(own_step.shape, step, jnp.float32)
    steps[place] = jnp.full(own_step.shape, step, jnp.float32)

    def put(field, slot):
        planes = lateral(field, x_pair, y_pair)
        for target in range(spaces):
            for c in range(chunks):
                low = (target * chunks + c) * rows
                for z in range(depth):
                    in_send[c, target, slot, z] = planes[z][low : low + rows]

    def keep(c, low, high):
        in_recv[c, me, low:high] = in_send[c, me, low:high]

    groups = ((0, 1), (1, 5), (5, 6))

    def in_copy(c, group, peer, source):
        low, high = groups[group]
        return pltpu.make_async_remote_copy(
            src_ref=in_send.at[c, peer, low:high],
            dst_ref=in_recv.at[c, source, low:high],
            send_sem=in_ss.at[c, group, peer],
            recv_sem=in_rs.at[c, group, source],
            device_id={"space": peer},
            device_id_type=MESH,
        )

    def in_start(c, group):
        for i in range(1, spaces):
            in_copy(c, group, lax.rem(me + i, spaces), me).start()

    def in_wait(c, group):
        for i in range(1, spaces):
            peer = lax.rem(me + i, spaces)
            in_copy(c, group, peer, peer).wait_recv()

    load_guess.wait()
    load_x.wait()
    load_y.wait()
    x_pair = (x_ref[0], x_ref[1])
    y_pair = (y_ref[0], y_ref[1])
    put(guess[...], 0)
    pl.semaphore_wait(barrier, spaces - 1 + slices - 1)
    for c in range(chunks):
        in_start(c, 0)

    def step_copy(peer, source):
        return pltpu.make_async_remote_copy(
            src_ref=own_step,
            dst_ref=steps.at[source],
            send_sem=s_ss.at[peer],
            recv_sem=s_rs.at[source],
            device_id={"tm": peer},
            device_id_type=MESH,
        )

    def peers(action):
        def one(i, carry):
            action(lax.rem(place + i, slices))
            return carry

        if slices > 8:
            lax.fori_loop(1, slices, one, 0)
        else:
            for i in range(1, slices):
                one(i, 0)


    for c in range(chunks):
        keep(c, 0, 1)
    load_initial.wait()

    @pl.when(place == 0)
    def _():
        put(initial[...], 5)
        for c in range(chunks):
            in_start(c, 2)
            keep(c, 5, 6)

    load_forcing.wait()
    for m in range(4):
        put(step * weighted(integrals[m], [forcing[j] for j in range(5)]), m + 1)
    for c in range(chunks):
        in_start(c, 1)
        keep(c, 1, 5)
    peers(lambda peer: step_copy(peer, place).start())

    z_eigen = eigen(length_z)
    load_lateral.wait()
    for c in range(chunks):
        low = pl.multiple_of((me * chunks + c) * rows, 8)
        base = lateral_ref[pl.ds(low, rows), :]
        for k in range(length_z):
            ell[c, k * rows : (k + 1) * rows] = -(base + float(z_eigen[k]))

    def table(i, carry):
        for c in range(chunks):
            at = pl.ds(pl.multiple_of(i * rows, 8), rows)
            gains, crossed = gains_of(step * ell[c, at])
            for m in range(1, 5):
                gain_c[c, m - 1, at] = gains[m]
                gain_d[c, m - 1, at] = crossed[m]
        return carry

    lax.fori_loop(0, length_z, table, 0, unroll=2)

    def planes_of(c, slot):
        return [in_recv[c, z // depth, slot, z % depth] for z in range(length_z)]

    def h_copy(c, peer):
        return pltpu.make_async_remote_copy(
            src_ref=ghat.at[c],
            dst_ref=hhat.at[c],
            send_sem=h_ss.at[c],
            recv_sem=h_rs.at[c],
            device_id={"tm": peer},
            device_id_type=MESH,
        )

    after = lax.rem(place + 1, slices)
    for c in range(chunks):
        in_wait(c, 0)
        for k, plane in enumerate(z_sine(planes_of(c, 0))):
            ghat[c, k * rows : (k + 1) * rows] = plane

        @pl.when(place < slices - 1)
        def _():
            h_copy(c, after).start()

    peers(lambda peer: step_copy(peer, peer).wait_recv())

    @pl.when(place < owners)
    def _():
        def one(p, carry):
            for c in range(chunks):
                at = pl.ds(pl.multiple_of(place * block, 8), block)
                gains, crossed = gains_of(steps[p][0:1] * ell[c, at])
                own_gain[c, p] = gains[4]
                own_cross[c, p] = crossed[4]
            return carry

        lax.fori_loop(0, slices, one, 0, unroll=2)

    def z_copy(c, owner, source):
        return pltpu.make_async_remote_copy(
            src_ref=z_send.at[c, owner],
            dst_ref=z_recv.at[c, source],
            send_sem=z_ss.at[c],
            recv_sem=z_rs.at[c],
            device_id={"tm": owner},
            device_id_type=MESH,
        )

    def to_owner(owner, action):
        if owners == slices:
            action()
        else:
            pl.when(owner < owners)(action)

    def bulk_wait(ref, sem, count):
        pltpu.make_async_copy(ref.at[0:count], ref.at[0:count], sem).wait()

    def owner_wait(ref, sem):
        if owners == slices:
            bulk_wait(ref, sem, owners - 1)
        else:
            pl.when(place < owners)(lambda: bulk_wait(ref, sem, owners - 1))
            pl.when(place >= owners)(lambda: bulk_wait(ref, sem, owners))

    first = jnp.where(place == 0, 1.0, 0.0).astype(jnp.float32)
    for c in range(chunks):
        in_wait(c, 1)
        fhat = [z_sine(planes_of(c, m + 1)) for m in range(4)]
        for m in range(4):
            for k in range(length_z):
                part_b[c, m, k * rows : (k + 1) * rows] = fhat[m][k]

        @pl.when(place == 0)
        def _():
            in_wait(c, 2)
            for k, plane in enumerate(z_sine(planes_of(c, 5))):
                hhat[c, k * rows : (k + 1) * rows] = plane

        @pl.when(place > 0)
        def _():
            h_copy(c, after).wait_recv()

        def solve(i, carry):
            at = pl.ds(pl.multiple_of(i * block, 8), block)
            rate = step * ell[c, at]
            middle = 1.0 + 0.5 * rate
            guess_hat, start = ghat[c, at], hhat[c, at]
            sources = [part_b[c, m, at] for m in range(4)]
            one = sweep(rate, [start] + [guess_hat] * 4, sources)
            nodes = corrected(*one, middle)
            rest = corrected(*sweep(rate, nodes, sources), middle)
            for m in range(1, 5):
                part_b[c, m - 1, at] = rest[m]
            seen = first * start
            gain, cross = gain_c[c, 3, at], gain_d[c, 3, at]
            z_send[c, i, 0] = nodes[4] + gain * seen
            z_send[c, i, 1] = rest[4] + (gain + cross) * seen
            return carry

        lax.fori_loop(0, owners, solve, 0, unroll=4)
        peers(lambda peer: to_owner(peer, lambda: z_copy(c, peer, place).start()))

        @pl.when(place < owners)
        def _():
            z_recv[c, place] = z_send[c, place]

    def r_copy(c, target, owner):
        return pltpu.make_async_remote_copy(
            src_ref=r_send.at[c, target],
            dst_ref=r_recv.at[c, owner],
            send_sem=r_ss.at[c],
            recv_sem=r_rs.at[c],
            device_id={"tm": target},
            device_id_type=MESH,
        )

    for c in range(chunks):
        @pl.when(place < owners)
        def _():
            bulk_wait(z_recv.at[c], z_rs.at[c], slices - 1)

            def scan(p, state):
                lower, upper = state
                r_send[c, p, 0] = lower
                r_send[c, p, 1] = upper
                gain = own_gain[c, p]
                return (
                    gain * lower + z_recv[c, p, 0],
                    gain * upper + own_cross[c, p] * lower + z_recv[c, p, 1],
                )

            zero = jnp.zeros((block, width_y), jnp.float32)
            lax.fori_loop(0, slices, scan, (zero, zero), unroll=8)
            peers(lambda peer: r_copy(c, peer, place).start())
            r_recv[c, place] = r_send[c, place]

    def o_groups(c):
        return ((0, 3), (3, 5)) if c == chunks - 1 else ((0, 5),)

    def o_copy(c, group, peer, source):
        low, high = o_groups(c)[group]
        return pltpu.make_async_remote_copy(
            src_ref=o_send.at[c, peer, low:high],
            dst_ref=o_recv.at[c, source, low:high],
            send_sem=o_ss.at[c, group, peer],
            recv_sem=o_rs.at[c, group, source],
            device_id={"space": peer},
            device_id_type=MESH,
        )

    for c in range(chunks):
        owner_wait(r_recv.at[c], r_rs.at[c])
        own = hhat[c].reshape(owners, block, width_y)
        lower = jnp.where(place == 0, own, r_recv[c, :, 0]).reshape(length_z * rows, width_y)
        upper = jnp.where(place == 0, own, r_recv[c, :, 1]).reshape(length_z * rows, width_y)
        for m in range(5):
            if m == 0:
                value = upper
            else:
                value = (
                    gain_c[c, m - 1] * upper + gain_d[c, m - 1] * lower + part_b[c, m - 1]
                )
            planes = z_sine([value[k * rows : (k + 1) * rows] for k in range(length_z)])
            for z in range(length_z):
                o_send[c, z // depth, m, z % depth] = planes[z]
            for group, (_, high) in enumerate(o_groups(c)):
                if high == m + 1:
                    for i in range(1, spaces):
                        o_copy(c, group, lax.rem(me + i, spaces), me).start()
            o_recv[c, me, m] = o_send[c, me, m]

    for c in range(chunks):
        for i in range(1, spaces):
            peer = lax.rem(me + i, spaces)
            in_copy(c, 0, peer, me).wait_send()
            in_copy(c, 1, peer, me).wait_send()

        @pl.when(place == 0)
        def _():
            for i in range(1, spaces):
                in_copy(c, 2, lax.rem(me + i, spaces), me).wait_send()

        @pl.when(place < slices - 1)
        def _():
            h_copy(c, after).wait_send()

        owner_wait(z_send.at[c], z_ss.at[c])

        @pl.when(place < owners)
        def _():
            bulk_wait(r_send.at[c], r_ss.at[c], slices - 1)

    peers(lambda peer: step_copy(peer, place).wait_send())

    for m in range(5):
        for c in range(chunks):
            for group, (low, _) in enumerate(o_groups(c)):
                if low == m:
                    for i in range(1, spaces):
                        peer = lax.rem(me + i, spaces)
                        o_copy(c, group, peer, peer).wait_recv()
        field = jnp.stack(
            [
                jnp.concatenate(
                    [o_recv[c, s, m, z] for s in range(spaces) for c in range(chunks)], axis=0
                )
                for z in range(depth)
            ]
        )
        planes = lateral(field, x_pair, y_pair)
        for z in range(depth):
            result_ref[0, m, z] = planes[z]

    for c in range(chunks):
        for i in range(1, spaces):
            for group in range(len(o_groups(c))):
                o_copy(c, group, lax.rem(me + i, spaces), me).wait_send()


def body(initial, start_guess, forcing, step_size):
    depth, width_x, width_y = initial.shape
    spaces, slices = lax.axis_size("space"), lax.axis_size("tm")
    length_z = depth * spaces
    chunks = CHUNKS
    rows = width_x // spaces // chunks
    owners = min(slices, length_z * rows // 8)
    block = length_z * rows // owners
    dims = (spaces, slices, chunks, depth, length_z, rows, width_y, owners, block)

    def pair(length):
        full = jnp.asarray(sine(length), jnp.float32)
        return jnp.stack(split_pair(full))

    sides = jnp.asarray(eigen(width_x)[:, None] + eigen(width_y)[None, :], jnp.float32)
    f32 = jnp.float32
    flat = length_z * rows
    dma = pltpu.SemaphoreType.DMA
    vmem = pl.BlockSpec(memory_space=pltpu.VMEM)
    hbm = pl.BlockSpec(memory_space=pl.ANY)
    return pl.pallas_call(
        functools.partial(kernel, dims),
        out_shape=pltpu.VMEM((1, 5, depth, width_x, width_y), f32),
        in_specs=[pl.BlockSpec(memory_space=pltpu.SMEM), hbm, hbm, hbm, hbm, hbm, hbm],
        out_specs=vmem,
        scratch_shapes=[
            pltpu.VMEM((depth, width_x, width_y), f32),
            pltpu.VMEM((depth, width_x, width_y), f32),
            pltpu.VMEM((5, depth, width_x, width_y), f32),
            pltpu.VMEM((2, width_x, width_x), jnp.bfloat16),
            pltpu.VMEM((2, width_y, width_y), jnp.bfloat16),
            pltpu.VMEM((width_x, width_y), f32),
            pltpu.VMEM((chunks, spaces, 6, depth, rows, width_y), f32),
            pltpu.VMEM((chunks, spaces, 6, depth, rows, width_y), f32),
            pltpu.VMEM((chunks, flat, width_y), f32),
            pltpu.VMEM((chunks, flat, width_y), f32),
            pltpu.VMEM((chunks, flat, width_y), f32),
            pltpu.VMEM((8, width_y), f32),
            pltpu.VMEM((slices, 8, width_y), f32),
            pltpu.VMEM((chunks, 4, flat, width_y), f32),
            pltpu.VMEM((chunks, 4, flat, width_y), f32),
            pltpu.VMEM((chunks, 4, flat, width_y), f32),
            pltpu.VMEM((chunks, owners, 2, block, width_y), f32),
            pltpu.VMEM((chunks, slices, 2, block, width_y), f32),
            pltpu.VMEM((chunks, slices, block, width_y), f32),
            pltpu.VMEM((chunks, slices, block, width_y), f32),
            pltpu.VMEM((chunks, slices, 2, block, width_y), f32),
            pltpu.VMEM((chunks, owners, 2, block, width_y), f32),
            pltpu.VMEM((chunks, spaces, 5, depth, rows, width_y), f32),
            pltpu.VMEM((chunks, spaces, 5, depth, rows, width_y), f32),
            dma((6,)),
            dma((chunks, 3, spaces)),
            dma((chunks, 3, spaces)),
            dma((chunks,)),
            dma((chunks,)),
            dma((slices,)),
            dma((slices,)),
            dma((chunks,)),
            dma((chunks,)),
            dma((chunks,)),
            dma((chunks,)),
            dma((chunks, 5, spaces)),
            dma((chunks, 5, spaces)),
        ],
        compiler_params=pltpu.CompilerParams(collective_id=0, has_side_effects=True),
    )(step_size, initial, start_guess, forcing, pair(width_x), pair(width_y), sides)


def solution(mesh):
    in_specs = (
        P("space", None, None),
        P("tm", "space", None, None),
        P("tm", None, "space", None, None),
        P("tm"),
    )
    out_specs = P("tm", None, "space", None, None)
    return jax.shard_map(body, mesh=mesh, in_specs=in_specs, out_specs=out_specs, check_vma=False)
```

profile of v0, /device:TPU:0, one launch (start us, length us, event | category | flops | bytes accessed | tf_op | source)
XLA Modules:
  0.0 34.7 jit_solution(4531539238493525374)
XLA Ops:
  0.7 33.2 %shard_map.73 = f32[1,5,2,128,128]{4,3,2,1,0:T(8,128)S(1)} custom-call(f32[1]{0:T(128)S(6)} %copy.10.step_ref, f32[2,128,128]{2,1,0:T(8,128)} %initial_hbm.1, f32[1,2,128,128]{3,2,1,0:T(8,128)} %guess_hbm.1, f32[1,5,2,128,128]{4,3,2,1,0:T(8,128)} %forcing_hbm.1, bf16[2,128,128]{2,1,0:T(8,128)(2,1)} %constant.16.x_hbm.y_hbm, ...), custom_call_target="tpu_custom_call" | custom-call | tf_op jit(solution)/shard_map/pallas_call | solution.py:572
  33.9 0.8 %copy.9 = f32[1,5,2,128,128]{4,3,2,1,0:T(8,128)} copy(f32[1,5,2,128,128]{4,3,2,1,0:T(8,128)S(1)} %shard_map.73) | data formatting | bytes 1310720
where the time goes:
time: 34.9 us; the launch traced here: 34.7 us
  Pallas kernels  33.2 us (95%)
  local copies, waits for them, and re-layouts  0.84 us (2%)
  between operations  0.66 us (2%)
    pallas_call x1, Pallas kernels, body(): pl.pallas_call(functools.partial(kernel, dims), out_shape=pltpu.VMEM((1,...  33.2 us
    unnamed x1, local copies, waits for them, and re-layouts  0.84 us

commit v1 on v0

--- a/solution.py
+++ b/solution.py
@@ -10,8 +10,8 @@
 from jax.sharding import PartitionSpec as P
 
 MESH = pl.DeviceIdType.MESH
-CHUNKS = 2
-
+CHUNKS = 4
+UNROLL = 8
 
 def node_tables():
     radical = math.sqrt(3.0 / 7.0)
@@ -76,16 +76,23 @@
     return jnp.dot(a, b, preferred_element_type=jnp.float32)
 
 
-def precise(a, b):
-    return dot(a[0], b[0]) + (dot(a[1], b[0]) + dot(a[0], b[1]))
-
-
-def lateral(field, x_pair, y_pair):
+def along_y(field, w_ref):
+    width = field.shape[1]
+    both = dot(jnp.concatenate(split_pair(field), axis=1), w_ref[...])
+    return both[:, :width] + both[:, width:]
+
+
+def along_x(pair, high, x_ref, low_ref):
+    return dot(x_ref[...], pair) + dot(low_ref[...], high)
+
+
+def lateral(field, x_ref, low_ref, w_ref):
     depth, width_x, width_y = field.shape
-    mixed = precise(split_pair(field.reshape(depth * width_x, width_y)), y_pair)
-    return [
-        precise(x_pair, split_pair(mixed[z * width_x : (z + 1) * width_x])) for z in range(depth)
-    ]
+    mixed = along_y(field.reshape(depth * width_x, width_y), w_ref)
+    mixed = jnp.concatenate([mixed[z * width_x : (z + 1) * width_x] for z in range(depth)], axis=1)
+    high, low = split_pair(mixed)
+    out = along_x(jnp.concatenate([high, low], axis=0), high, x_ref, low_ref)
+    return [out[:, z * width_y : (z + 1) * width_y] for z in range(depth)]
 
 
 def z_sine(planes):
@@ -185,54 +192,56 @@
 
 def kernel(
     dims,
-    step_ref, initial_hbm, guess_hbm, forcing_hbm, x_hbm, y_hbm, lateral_hbm,
+    step_ref, initial_hbm, guess_hbm, forcing_hbm, x_hbm, low_hbm, w_hbm, lateral_hbm,
     result_ref,
-    initial, guess, forcing, x_ref, y_ref, lateral_ref,
+    initial, guess, forcing, x_ref, low_ref, w_ref, lateral_ref,
     in_send, in_recv, ghat, hhat, ell, own_step, steps,
     gain_c, gain_d, part_b, z_send, z_recv, own_gain, own_cross, r_send, r_recv,
-    o_send, o_recv,
+    o_send, o_recv, mix,
     load_sem, in_ss, in_rs, h_ss, h_rs, s_ss, s_rs, z_ss, z_rs, r_ss, r_rs, o_ss, o_rs,
+    near_sem, next_sem, open_sem,
 ):
     spaces, slices, chunks, depth, length_z, rows, width_y, owners, block = dims
     me = lax.axis_index("space")
     place = lax.axis_index("tm")
     _, integrals, _ = TABLES
     width_x = spaces * chunks * rows
+    everyone = spaces - 2
 
     barrier = pltpu.get_barrier_semaphore()
+    odd = lax.rem(me, 2) == 1
     for i in range(1, spaces):
-        pl.semaphore_signal(
-            barrier, inc=1, device_id={"space": lax.rem(me + i, spaces)}, device_id_type=MESH
-        )
-
-    def greet(i, carry):
-        pl.semaphore_signal(
-            barrier, inc=1, device_id={"tm": lax.rem(place + i, slices)}, device_id_type=MESH
-        )
-        return carry
-
-    lax.fori_loop(1, slices, greet, 0)
-
-    sources = (guess_hbm.at[0], x_hbm, y_hbm, forcing_hbm.at[0], initial_hbm, lateral_hbm)
+        peer = lax.rem(me + i, spaces)
+
+        @pl.when(lax.rem(peer, 2) == 1)
+        def _():
+            pl.semaphore_signal(barrier, inc=1, device_id={"space": peer}, device_id_type=MESH)
+
+    sources = (
+        guess_hbm.at[0], w_hbm, x_hbm, low_hbm, forcing_hbm.at[0], initial_hbm, lateral_hbm
+    )
     loads = [
         pltpu.make_async_copy(source, target, load_sem.at[i])
         for i, (source, target) in enumerate(
-            zip(sources, (guess, x_ref, y_ref, forcing, initial, lateral_ref))
+            zip(sources, (guess, w_ref, x_ref, low_ref, forcing, initial, lateral_ref))
         )
     ]
     for load in loads:
         load.start()
-    load_guess, load_x, load_y, load_forcing, load_initial, load_lateral = loads
+    load_guess, load_w, load_x, load_low, load_forcing, load_initial, load_lateral = loads
 
     step = step_ref[0]
     own_step[...] = jnp.full(own_step.shape, step, jnp.float32)
     steps[place] = jnp.full(own_step.shape, step, jnp.float32)
 
+    def low_of(c, s):
+        return (c * spaces + s) * rows
+
     def put(field, slot):
-        planes = lateral(field, x_pair, y_pair)
+        planes = lateral(field, x_ref, low_ref, w_ref)
         for target in range(spaces):
             for c in range(chunks):
-                low = (target * chunks + c) * rows
+                low = low_of(c, target)
                 for z in range(depth):
                     in_send[c, target, slot, z] = planes[z][low : low + rows]
 
@@ -262,14 +271,133 @@
             in_copy(c, group, peer, peer).wait_recv()
 
     load_guess.wait()
+    load_w.wait()
     load_x.wait()
-    load_y.wait()
-    x_pair = (x_ref[0], x_ref[1])
-    y_pair = (y_ref[0], y_ref[1])
+    load_low.wait()
     put(guess[...], 0)
-    pl.semaphore_wait(barrier, spaces - 1 + slices - 1)
+
+    @pl.when(odd)
+    def _():
+        pl.semaphore_wait(barrier, spaces - 1)
+        pl.semaphore_signal(near_sem, inc=1, device_id={"space": me - 1}, device_id_type=MESH)
+
+    @pl.when(jnp.logical_not(odd))
+    def _():
+        pl.semaphore_wait(near_sem, 1)
+
+    for c in range(min(2, chunks)):
+        in_start(c, 0)
+
+    @pl.when(jnp.logical_and(me == 0, place > 0))
+    def _():
+        pl.semaphore_signal(barrier, inc=1, device_id={"tm": place - 1}, device_id_type=MESH)
+
+    def peers(action):
+        def one(i, carry):
+            action(lax.rem(place + i, slices))
+            return carry
+
+        if slices > UNROLL:
+            lax.fori_loop(1, slices, one, 0)
+        else:
+            for i in range(1, slices):
+                one(i, 0)
+
+    @pl.when(me == everyone)
+    def _():
+        peers(
+            lambda peer: pl.semaphore_signal(
+                barrier, inc=1, device_id={"tm": peer}, device_id_type=MESH
+            )
+        )
+
+    def tell(sem):
+        for i in range(1, spaces):
+            pl.semaphore_signal(
+                sem, inc=1, device_id={"space": lax.rem(me + i, spaces)}, device_id_type=MESH
+            )
+
     for c in range(chunks):
-        in_start(c, 0)
+        keep(c, 0, 1)
+    load_forcing.wait()
+    for m in range(4):
+        put(step * weighted(integrals[m], [forcing[j] for j in range(5)]), m + 1)
+
+    load_initial.wait()
+
+    @pl.when(place == 0)
+    def _():
+        put(initial[...], 5)
+
+    for c in range(chunks):
+        in_start(c, 1)
+
+        @pl.when(place == 0)
+        def _():
+            in_start(c, 2)
+
+        if c + 2 < chunks:
+            in_start(c + 2, 0)
+    for c in range(chunks):
+        keep(c, 1, 5)
+
+        @pl.when(place == 0)
+        def _():
+            keep(c, 5, 6)
+
+    @pl.when(place < slices - 1)
+    def _():
+        @pl.when(me == 0)
+        def _():
+            pl.semaphore_wait(barrier, 1)
+            tell(next_sem)
+
+    z_eigen = eigen(length_z)
+    load_lateral.wait()
+    for c in range(chunks):
+        low = pl.multiple_of(low_of(c, me), 8)
+        base = lateral_ref[pl.ds(low, rows), :]
+        for k in range(length_z):
+            ell[c, k * rows : (k + 1) * rows] = -(base + float(z_eigen[k]))
+
+    def table(i, carry):
+        for c in range(chunks):
+            at = pl.ds(pl.multiple_of(i * rows, 8), rows)
+            gains, crossed = gains_of(step * ell[c, at])
+            for m in range(1, 5):
+                gain_c[c, m - 1, at] = gains[m]
+                gain_d[c, m - 1, at] = crossed[m]
+        return carry
+
+    lax.fori_loop(0, length_z, table, 0)
+
+    def planes_of(c, slot):
+        return [in_recv[c, z // depth, slot, z % depth] for z in range(length_z)]
+
+    def h_copy(c, peer):
+        return pltpu.make_async_remote_copy(
+            src_ref=ghat.at[c],
+            dst_ref=hhat.at[c],
+            send_sem=h_ss.at[c],
+            recv_sem=h_rs.at[c],
+            device_id={"tm": peer},
+            device_id_type=MESH,
+        )
+
+    after = lax.rem(place + 1, slices)
+
+    def hand(c):
+        in_wait(c, 0)
+        for k, plane in enumerate(z_sine(planes_of(c, 0))):
+            ghat[c, k * rows : (k + 1) * rows] = plane
+
+        @pl.when(place < slices - 1)
+        def _():
+            h_copy(c, after).start()
+
+    @pl.when(jnp.logical_and(place < slices - 1, me != 0))
+    def _():
+        pl.semaphore_wait(next_sem, 1)
 
     def step_copy(peer, source):
         return pltpu.make_async_remote_copy(
@@ -281,99 +409,12 @@
             device_id_type=MESH,
         )
 
-    def peers(action):
-        def one(i, carry):
-            action(lax.rem(place + i, slices))
-            return carry
-
-        if slices > 8:
-            lax.fori_loop(1, slices, one, 0)
-        else:
-            for i in range(1, slices):
-                one(i, 0)
-
-
-    for c in range(chunks):
-        keep(c, 0, 1)
-    load_initial.wait()
-
-    @pl.when(place == 0)
-    def _():
-        put(initial[...], 5)
-        for c in range(chunks):
-            in_start(c, 2)
-            keep(c, 5, 6)
-
-    load_forcing.wait()
-    for m in range(4):
-        put(step * weighted(integrals[m], [forcing[j] for j in range(5)]), m + 1)
-    for c in range(chunks):
-        in_start(c, 1)
-        keep(c, 1, 5)
-    peers(lambda peer: step_copy(peer, place).start())
-
-    z_eigen = eigen(length_z)
-    load_lateral.wait()
-    for c in range(chunks):
-        low = pl.multiple_of((me * chunks + c) * rows, 8)
-        base = lateral_ref[pl.ds(low, rows), :]
-        for k in range(length_z):
-            ell[c, k * rows : (k + 1) * rows] = -(base + float(z_eigen[k]))
-
-    def table(i, carry):
-        for c in range(chunks):
-            at = pl.ds(pl.multiple_of(i * rows, 8), rows)
-            gains, crossed = gains_of(step * ell[c, at])
-            for m in range(1, 5):
-                gain_c[c, m - 1, at] = gains[m]
-                gain_d[c, m - 1, at] = crossed[m]
-        return carry
-
-    lax.fori_loop(0, length_z, table, 0, unroll=2)
-
-    def planes_of(c, slot):
-        return [in_recv[c, z // depth, slot, z % depth] for z in range(length_z)]
-
-    def h_copy(c, peer):
-        return pltpu.make_async_remote_copy(
-            src_ref=ghat.at[c],
-            dst_ref=hhat.at[c],
-            send_sem=h_ss.at[c],
-            recv_sem=h_rs.at[c],
-            device_id={"tm": peer},
-            device_id_type=MESH,
-        )
-
-    after = lax.rem(place + 1, slices)
-    for c in range(chunks):
-        in_wait(c, 0)
-        for k, plane in enumerate(z_sine(planes_of(c, 0))):
-            ghat[c, k * rows : (k + 1) * rows] = plane
-
-        @pl.when(place < slices - 1)
-        def _():
-            h_copy(c, after).start()
-
-    peers(lambda peer: step_copy(peer, peer).wait_recv())
-
-    @pl.when(place < owners)
-    def _():
-        def one(p, carry):
-            for c in range(chunks):
-                at = pl.ds(pl.multiple_of(place * block, 8), block)
-                gains, crossed = gains_of(steps[p][0:1] * ell[c, at])
-                own_gain[c, p] = gains[4]
-                own_cross[c, p] = crossed[4]
-            return carry
-
-        lax.fori_loop(0, slices, one, 0, unroll=2)
-
     def z_copy(c, owner, source):
         return pltpu.make_async_remote_copy(
             src_ref=z_send.at[c, owner],
             dst_ref=z_recv.at[c, source],
             send_sem=z_ss.at[c],
-            recv_sem=z_rs.at[c],
+            recv_sem=z_rs.at[c, source],
             device_id={"tm": owner},
             device_id_type=MESH,
         )
@@ -385,7 +426,8 @@
             pl.when(owner < owners)(action)
 
     def bulk_wait(ref, sem, count):
-        pltpu.make_async_copy(ref.at[0:count], ref.at[0:count], sem).wait()
+        if count > 0:
+            pltpu.make_async_copy(ref.at[0:count], ref.at[0:count], sem).wait()
 
     def owner_wait(ref, sem):
         if owners == slices:
@@ -394,8 +436,23 @@
             pl.when(place < owners)(lambda: bulk_wait(ref, sem, owners - 1))
             pl.when(place >= owners)(lambda: bulk_wait(ref, sem, owners))
 
+    def opened():
+        @pl.when(me == everyone)
+        def _():
+            pl.semaphore_wait(barrier, slices - 1)
+            tell(open_sem)
+
+        @pl.when(me != everyone)
+        def _():
+            pl.semaphore_wait(open_sem, 1)
+
+        peers(lambda peer: step_copy(peer, place).start())
+
     first = jnp.where(place == 0, 1.0, 0.0).astype(jnp.float32)
+    hand(0)
     for c in range(chunks):
+        if c + 1 < chunks:
+            hand(c + 1)
         in_wait(c, 1)
         fhat = [z_sine(planes_of(c, m + 1)) for m in range(4)]
         for m in range(4):
@@ -430,11 +487,30 @@
             return carry
 
         lax.fori_loop(0, owners, solve, 0, unroll=4)
-        peers(lambda peer: to_owner(peer, lambda: z_copy(c, peer, place).start()))
+        if c == 0:
+            opened()
+
+        @pl.when(place < slices - 1)
+        def _():
+            peers(lambda peer: to_owner(peer, lambda: z_copy(c, peer, place).start()))
 
         @pl.when(place < owners)
         def _():
             z_recv[c, place] = z_send[c, place]
+
+    peers(lambda peer: step_copy(peer, peer).wait_recv())
+
+    @pl.when(place < owners)
+    def _():
+        def one(p, carry):
+            for c in range(chunks):
+                at = pl.ds(pl.multiple_of(place * block, 8), block)
+                gains, crossed = gains_of(steps[p][0:1] * ell[c, at])
+                own_gain[c, p] = gains[4]
+                own_cross[c, p] = crossed[4]
+            return carry
+
+        lax.fori_loop(0, slices - 1, one, 0)
 
     def r_copy(c, target, owner):
         return pltpu.make_async_remote_copy(
@@ -449,25 +525,42 @@
     for c in range(chunks):
         @pl.when(place < owners)
         def _():
-            bulk_wait(z_recv.at[c], z_rs.at[c], slices - 1)
-
             def scan(p, state):
+                @pl.when(p != place)
+                def _():
+                    z_copy(c, p, p).wait_recv()
+
                 lower, upper = state
-                r_send[c, p, 0] = lower
-                r_send[c, p, 1] = upper
                 gain = own_gain[c, p]
-                return (
+                lower, upper = (
                     gain * lower + z_recv[c, p, 0],
                     gain * upper + own_cross[c, p] * lower + z_recv[c, p, 1],
                 )
+                target = p + 1
+                r_send[c, target, 0] = lower
+                r_send[c, target, 1] = upper
+
+                @pl.when(target != place)
+                def _():
+                    r_copy(c, target, place).start()
+
+                @pl.when(target == place)
+                def _():
+                    r_recv[c, place, 0] = lower
+                    r_recv[c, place, 1] = upper
+
+                return lower, upper
 
             zero = jnp.zeros((block, width_y), jnp.float32)
-            lax.fori_loop(0, slices, scan, (zero, zero), unroll=8)
-            peers(lambda peer: r_copy(c, peer, place).start())
-            r_recv[c, place] = r_send[c, place]
+            state = (zero, zero)
+            if slices > UNROLL:
+                lax.fori_loop(0, slices - 1, scan, state)
+            else:
+                for p in range(slices - 1):
+                    state = scan(p, state)
 
     def o_groups(c):
-        return ((0, 3), (3, 5)) if c == chunks - 1 else ((0, 5),)
+        return tuple((m, m + 1) for m in range(5)) if c == chunks - 1 else ((0, 5),)
 
     def o_copy(c, group, peer, source):
         low, high = o_groups(c)[group]
@@ -480,8 +573,16 @@
             device_id_type=MESH,
         )
 
+    def o_wait(c, group):
+        for i in range(1, spaces):
+            peer = lax.rem(me + i, spaces)
+            o_copy(c, group, peer, peer).wait_recv()
+
     for c in range(chunks):
-        owner_wait(r_recv.at[c], r_rs.at[c])
+        @pl.when(place > 0)
+        def _():
+            owner_wait(r_recv.at[c], r_rs.at[c])
+
         own = hhat[c].reshape(owners, block, width_y)
         lower = jnp.where(place == 0, own, r_recv[c, :, 0]).reshape(length_z * rows, width_y)
         upper = jnp.where(place == 0, own, r_recv[c, :, 1]).reshape(length_z * rows, width_y)
@@ -501,6 +602,37 @@
                         o_copy(c, group, lax.rem(me + i, spaces), me).start()
             o_recv[c, me, m] = o_send[c, me, m]
 
+    def unmix(c, low, high):
+        stacked = jnp.concatenate(
+            [
+                o_recv[c, s, m, z]
+                for m in range(low, high)
+                for z in range(depth)
+                for s in range(spaces)
+            ],
+            axis=0,
+        )
+        tall = spaces * rows
+        mixed_high, mixed_low = split_pair(along_y(stacked, w_ref))
+        for m in range(low, high):
+            for z in range(depth):
+                at = ((m - low) * depth + z) * tall
+                lanes = slice(z * width_y, (z + 1) * width_y)
+                mix[m, c * tall : (c + 1) * tall, lanes] = mixed_high[at : at + tall]
+                mix[m, width_x + c * tall : width_x + (c + 1) * tall, lanes] = mixed_low[
+                    at : at + tall
+                ]
+
+    for c in range(chunks - 1):
+        o_wait(c, 0)
+        unmix(c, 0, 5)
+    for m in range(5):
+        o_wait(chunks - 1, m)
+        unmix(chunks - 1, m, m + 1)
+        out = along_x(mix[m], mix[m, :width_x], x_ref, low_ref)
+        for z in range(depth):
+            result_ref[0, m, z] = out[:, z * width_y : (z + 1) * width_y]
+
     for c in range(chunks):
         for i in range(1, spaces):
             peer = lax.rem(me + i, spaces)
@@ -515,38 +647,18 @@
         @pl.when(place < slices - 1)
         def _():
             h_copy(c, after).wait_send()
-
-        owner_wait(z_send.at[c], z_ss.at[c])
+            owner_wait(z_send.at[c], z_ss.at[c])
 
         @pl.when(place < owners)
         def _():
-            bulk_wait(r_send.at[c], r_ss.at[c], slices - 1)
-
-    peers(lambda peer: step_copy(peer, place).wait_send())
-
-    for m in range(5):
-        for c in range(chunks):
-            for group, (low, _) in enumerate(o_groups(c)):
-                if low == m:
-                    for i in range(1, spaces):
-                        peer = lax.rem(me + i, spaces)
-                        o_copy(c, group, peer, peer).wait_recv()
-        field = jnp.stack(
-            [
-                jnp.concatenate(
-                    [o_recv[c, s, m, z] for s in range(spaces) for c in range(chunks)], axis=0
-                )
-                for z in range(depth)
-            ]
-        )
-        planes = lateral(field, x_pair, y_pair)
-        for z in range(depth):
-            result_ref[0, m, z] = planes[z]
-
-    for c in range(chunks):
+            pl.when(place == 0)(lambda: bulk_wait(r_send.at[c], r_ss.at[c], slices - 1))
+            pl.when(place > 0)(lambda: bulk_wait(r_send.at[c], r_ss.at[c], slices - 2))
+
         for i in range(1, spaces):
             for group in range(len(o_groups(c))):
                 o_copy(c, group, lax.rem(me + i, spaces), me).wait_send()
+
+    peers(lambda peer: step_copy(peer, place).wait_send())
 
 
 def body(initial, start_guess, forcing, step_size):
@@ -560,26 +672,37 @@
     dims = (spaces, slices, chunks, depth, length_z, rows, width_y, owners, block)
 
     def pair(length):
-        full = jnp.asarray(sine(length), jnp.float32)
-        return jnp.stack(split_pair(full))
-
+        return split_pair(jnp.asarray(sine(length), jnp.float32))
+
+    x_high, x_low = pair(width_x)
+    y_high, y_low = pair(width_y)
+    x_twice = jnp.concatenate([x_high, x_high], axis=1)
+    w = jnp.concatenate(
+        [
+            jnp.concatenate([y_high, y_low], axis=1),
+            jnp.concatenate([y_high, jnp.zeros_like(y_low)], axis=1),
+        ],
+        axis=0,
+    )
     sides = jnp.asarray(eigen(width_x)[:, None] + eigen(width_y)[None, :], jnp.float32)
-    f32 = jnp.float32
+    f32, b16 = jnp.float32, jnp.bfloat16
     flat = length_z * rows
     dma = pltpu.SemaphoreType.DMA
+    regular = pltpu.SemaphoreType.REGULAR
     vmem = pl.BlockSpec(memory_space=pltpu.VMEM)
     hbm = pl.BlockSpec(memory_space=pl.ANY)
     return pl.pallas_call(
         functools.partial(kernel, dims),
         out_shape=pltpu.VMEM((1, 5, depth, width_x, width_y), f32),
-        in_specs=[pl.BlockSpec(memory_space=pltpu.SMEM), hbm, hbm, hbm, hbm, hbm, hbm],
+        in_specs=[pl.BlockSpec(memory_space=pltpu.SMEM)] + [hbm] * 7,
         out_specs=vmem,
         scratch_shapes=[
             pltpu.VMEM((depth, width_x, width_y), f32),
             pltpu.VMEM((depth, width_x, width_y), f32),
             pltpu.VMEM((5, depth, width_x, width_y), f32),
-            pltpu.VMEM((2, width_x, width_x), jnp.bfloat16),
-            pltpu.VMEM((2, width_y, width_y), jnp.bfloat16),
+            pltpu.VMEM((width_x, 2 * width_x), b16),
+            pltpu.VMEM((width_x, width_x), b16),
+            pltpu.VMEM((2 * width_y, 2 * width_y), b16),
             pltpu.VMEM((width_x, width_y), f32),
             pltpu.VMEM((chunks, spaces, 6, depth, rows, width_y), f32),
             pltpu.VMEM((chunks, spaces, 6, depth, rows, width_y), f32),
@@ -599,7 +722,8 @@
             pltpu.VMEM((chunks, owners, 2, block, width_y), f32),
             pltpu.VMEM((chunks, spaces, 5, depth, rows, width_y), f32),
             pltpu.VMEM((chunks, spaces, 5, depth, rows, width_y), f32),
-            dma((6,)),
+            pltpu.VMEM((5, 2 * width_x, depth * width_y), b16),
+            dma((7,)),
             dma((chunks, 3, spaces)),
             dma((chunks, 3, spaces)),
             dma((chunks,)),
@@ -607,14 +731,17 @@
             dma((slices,)),
             dma((slices,)),
             dma((chunks,)),
-            dma((chunks,)),
+            dma((chunks, slices)),
             dma((chunks,)),
             dma((chunks,)),
             dma((chunks, 5, spaces)),
             dma((chunks, 5, spaces)),
+            regular,
+            regular,
+            regular,
         ],
         compiler_params=pltpu.CompilerParams(collective_id=0, has_side_effects=True),
-    )(step_size, initial, start_guess, forcing, pair(width_x), pair(width_y), sides)
+    )(step_size, initial, start_guess, forcing, x_twice, x_low, w, sides)
 
 
 def solution(mesh):

time: 34.9 us -> 36.9 us (1.057)
  Pallas kernels: 33.2 us -> 35.2 us
    pallas_call x1, Pallas kernels: 33.2 us -> 35.2 us  [body(): pl.pallas_call(functools.partial(kernel, dims), out_shape=pltpu.VMEM((1,...]
where the time goes in v1:
time: 36.9 us; the launch traced here: 36.7 us
  Pallas kernels  35.2 us (95%)
  local copies, waits for them, and re-layouts  0.84 us (2%)
  between operations  0.66 us (2%)
    pallas_call x1, Pallas kernels, body(): pl.pallas_call(functools.partial(kernel, dims), out_shape=pltpu.VMEM((1,...  35.2 us
    unnamed x1, local copies, waits for them, and re-layouts  0.84 us

profile of v1, /device:TPU:0, one launch (start us, length us, event | category | flops | bytes accessed | tf_op | source)
XLA Modules:
  0.0 36.7 jit_solution(5524532097333155890)
XLA Ops:
  0.7 35.2 %shard_map.73 = f32[1,5,2,128,128]{4,3,2,1,0:T(8,128)S(1)} custom-call(f32[1]{0:T(128)S(6)} %copy.10.step_ref, f32[2,128,128]{2,1,0:T(8,128)} %initial_hbm.1, f32[1,2,128,128]{3,2,1,0:T(8,128)} %guess_hbm.1, f32[1,5,2,128,128]{4,3,2,1,0:T(8,128)} %forcing_hbm.1, bf16[128,256]{1,0:T(8,128)(2,1)} %constant.15.x_hbm, bf16[128,128]{1,0:T(8,128)(2,1)} %constant.18.low_hbm, ...), custom_call_target="tpu_custom_call" | custom-call | tf_op jit(solution)/shard_map/pallas_call | solution.py:694
  35.9 0.8 %copy.9 = f32[1,5,2,128,128]{4,3,2,1,0:T(8,128)} copy(f32[1,5,2,128,128]{4,3,2,1,0:T(8,128)S(1)} %shard_map.73) | data formatting | bytes 1310720

commit v2 on v1

--- a/solution.py
+++ b/solution.py
@@ -11,7 +11,7 @@
 
 MESH = pl.DeviceIdType.MESH
 CHUNKS = 4
-UNROLL = 8
+GROUP = 8
 
 def node_tables():
     radical = math.sqrt(3.0 / 7.0)
@@ -197,16 +197,20 @@
     initial, guess, forcing, x_ref, low_ref, w_ref, lateral_ref,
     in_send, in_recv, ghat, hhat, ell, own_step, steps,
     gain_c, gain_d, part_b, z_send, z_recv, own_gain, own_cross, r_send, r_recv,
-    o_send, o_recv, mix,
-    load_sem, in_ss, in_rs, h_ss, h_rs, s_ss, s_rs, z_ss, z_rs, r_ss, r_rs, o_ss, o_rs,
-    near_sem, next_sem, open_sem,
+    s_send, s_recv, o_send, o_recv, mix,
+    load_sem, in_rs, h_rs, z_rs, s_rs, r_rs, o_rs, sent, signals,
 ):
-    spaces, slices, chunks, depth, length_z, rows, width_y, owners, block = dims
+    spaces, slices, chunks, depth, length_z, rows, width_y, group, block = dims
     me = lax.axis_index("space")
     place = lax.axis_index("tm")
     _, integrals, _ = TABLES
     width_x = spaces * chunks * rows
     everyone = spaces - 2
+    last_group = slices // group - 1
+    family, mine = place // group, lax.rem(place, group)
+    eldest = place - mine
+    near_sem, next_sem, open_sem = (signals.at[i] for i in range(3))
+    in_ss, h_ss, step_ss, z_ss, s_ss, r_ss, o_ss, step_rs = (sent.at[i] for i in range(8))
 
     barrier = pltpu.get_barrier_semaphore()
     odd = lax.rem(me, 2) == 1
@@ -232,7 +236,10 @@
 
     step = step_ref[0]
     own_step[...] = jnp.full(own_step.shape, step, jnp.float32)
-    steps[place] = jnp.full(own_step.shape, step, jnp.float32)
+    steps[mine] = jnp.full(own_step.shape, step, jnp.float32)
+
+    def bulk(ref, sem):
+        pltpu.make_async_copy(ref, ref, sem).wait()
 
     def low_of(c, s):
         return (c * spaces + s) * rows
@@ -248,27 +255,20 @@
     def keep(c, low, high):
         in_recv[c, me, low:high] = in_send[c, me, low:high]
 
-    groups = ((0, 1), (1, 5), (5, 6))
-
-    def in_copy(c, group, peer, source):
-        low, high = groups[group]
-        return pltpu.make_async_remote_copy(
-            src_ref=in_send.at[c, peer, low:high],
-            dst_ref=in_recv.at[c, source, low:high],
-            send_sem=in_ss.at[c, group, peer],
-            recv_sem=in_rs.at[c, group, source],
-            device_id={"space": peer},
-            device_id_type=MESH,
-        )
-
-    def in_start(c, group):
-        for i in range(1, spaces):
-            in_copy(c, group, lax.rem(me + i, spaces), me).start()
-
-    def in_wait(c, group):
+    def in_start(c, sem, low, high):
         for i in range(1, spaces):
             peer = lax.rem(me + i, spaces)
-            in_copy(c, group, peer, peer).wait_recv()
+            pltpu.make_async_remote_copy(
+                src_ref=in_send.at[c, peer, low:high],
+                dst_ref=in_recv.at[c, me, low:high],
+                send_sem=in_ss,
+                recv_sem=in_rs.at[c, sem],
+                device_id={"space": peer},
+                device_id_type=MESH,
+            ).start()
+
+    def in_wait(c, sem, low, high):
+        bulk(in_recv.at[c, 0 : spaces - 1, low:high], in_rs.at[c, sem])
 
     load_guess.wait()
     load_w.wait()
@@ -285,31 +285,24 @@
     def _():
         pl.semaphore_wait(near_sem, 1)
 
-    for c in range(min(2, chunks)):
-        in_start(c, 0)
+    for c in range(chunks):
+        in_start(c, 0, 0, 1)
 
     @pl.when(jnp.logical_and(me == 0, place > 0))
     def _():
         pl.semaphore_signal(barrier, inc=1, device_id={"tm": place - 1}, device_id_type=MESH)
 
-    def peers(action):
-        def one(i, carry):
-            action(lax.rem(place + i, slices))
-            return carry
-
-        if slices > UNROLL:
-            lax.fori_loop(1, slices, one, 0)
-        else:
-            for i in range(1, slices):
-                one(i, 0)
+    def relatives(action):
+        for i in range(1, group):
+            action(lax.rem(mine + i, group))
 
     @pl.when(me == everyone)
     def _():
-        peers(
-            lambda peer: pl.semaphore_signal(
-                barrier, inc=1, device_id={"tm": peer}, device_id_type=MESH
-            )
-        )
+        def greet(target):
+            pl.semaphore_signal(barrier, inc=1, device_id={"tm": target}, device_id_type=MESH)
+
+        relatives(lambda other: greet(eldest + other))
+        pl.when(family > 0)(lambda: greet(place - group))
 
     def tell(sem):
         for i in range(1, spaces):
@@ -328,29 +321,20 @@
     @pl.when(place == 0)
     def _():
         put(initial[...], 5)
-
-    for c in range(chunks):
-        in_start(c, 1)
-
-        @pl.when(place == 0)
-        def _():
-            in_start(c, 2)
-
-        if c + 2 < chunks:
-            in_start(c + 2, 0)
+        for c in range(chunks):
+            in_start(c, 1, 1, 6)
+
+    @pl.when(place > 0)
+    def _():
+        for c in range(chunks):
+            in_start(c, 1, 1, 5)
+
     for c in range(chunks):
         keep(c, 1, 5)
 
         @pl.when(place == 0)
         def _():
             keep(c, 5, 6)
-
-    @pl.when(place < slices - 1)
-    def _():
-        @pl.when(me == 0)
-        def _():
-            pl.semaphore_wait(barrier, 1)
-            tell(next_sem)
 
     z_eigen = eigen(length_z)
     load_lateral.wait()
@@ -374,100 +358,85 @@
     def planes_of(c, slot):
         return [in_recv[c, z // depth, slot, z % depth] for z in range(length_z)]
 
-    def h_copy(c, peer):
-        return pltpu.make_async_remote_copy(
-            src_ref=ghat.at[c],
-            dst_ref=hhat.at[c],
-            send_sem=h_ss.at[c],
-            recv_sem=h_rs.at[c],
-            device_id={"tm": peer},
-            device_id_type=MESH,
-        )
+    @pl.when(place < slices - 1)
+    def _():
+        @pl.when(me == 0)
+        def _():
+            pl.semaphore_wait(barrier, 1)
+            tell(next_sem)
+
+        @pl.when(me != 0)
+        def _():
+            pl.semaphore_wait(next_sem, 1)
 
     after = lax.rem(place + 1, slices)
-
-    def hand(c):
-        in_wait(c, 0)
+    for c in range(chunks):
+        in_wait(c, 0, 0, 1)
         for k, plane in enumerate(z_sine(planes_of(c, 0))):
             ghat[c, k * rows : (k + 1) * rows] = plane
 
         @pl.when(place < slices - 1)
         def _():
-            h_copy(c, after).start()
-
-    @pl.when(jnp.logical_and(place < slices - 1, me != 0))
-    def _():
-        pl.semaphore_wait(next_sem, 1)
-
-    def step_copy(peer, source):
-        return pltpu.make_async_remote_copy(
-            src_ref=own_step,
-            dst_ref=steps.at[source],
-            send_sem=s_ss.at[peer],
-            recv_sem=s_rs.at[source],
-            device_id={"tm": peer},
-            device_id_type=MESH,
-        )
-
-    def z_copy(c, owner, source):
-        return pltpu.make_async_remote_copy(
-            src_ref=z_send.at[c, owner],
-            dst_ref=z_recv.at[c, source],
-            send_sem=z_ss.at[c],
-            recv_sem=z_rs.at[c, source],
-            device_id={"tm": owner},
-            device_id_type=MESH,
-        )
-
-    def to_owner(owner, action):
-        if owners == slices:
-            action()
-        else:
-            pl.when(owner < owners)(action)
-
-    def bulk_wait(ref, sem, count):
-        if count > 0:
-            pltpu.make_async_copy(ref.at[0:count], ref.at[0:count], sem).wait()
-
-    def owner_wait(ref, sem):
-        if owners == slices:
-            bulk_wait(ref, sem, owners - 1)
-        else:
-            pl.when(place < owners)(lambda: bulk_wait(ref, sem, owners - 1))
-            pl.when(place >= owners)(lambda: bulk_wait(ref, sem, owners))
+            pltpu.make_async_remote_copy(
+                src_ref=ghat.at[c],
+                dst_ref=hhat.at[c],
+                send_sem=h_ss,
+                recv_sem=h_rs.at[c],
+                device_id={"tm": after},
+                device_id_type=MESH,
+            ).start()
 
     def opened():
         @pl.when(me == everyone)
         def _():
-            pl.semaphore_wait(barrier, slices - 1)
+            pl.when(family < last_group)(lambda: pl.semaphore_wait(barrier, group))
+            pl.when(family == last_group)(lambda: pl.semaphore_wait(barrier, group - 1))
             tell(open_sem)
 
         @pl.when(me != everyone)
         def _():
             pl.semaphore_wait(open_sem, 1)
 
-        peers(lambda peer: step_copy(peer, place).start())
+        relatives(
+            lambda other: pltpu.make_async_remote_copy(
+                src_ref=own_step,
+                dst_ref=steps.at[mine],
+                send_sem=step_ss,
+                recv_sem=step_rs,
+                device_id={"tm": eldest + other},
+                device_id_type=MESH,
+            ).start()
+        )
+
+    def z_start(c):
+        relatives(
+            lambda other: pltpu.make_async_remote_copy(
+                src_ref=z_send.at[c, other],
+                dst_ref=z_recv.at[c, mine],
+                send_sem=z_ss,
+                recv_sem=z_rs.at[c],
+                device_id={"tm": eldest + other},
+                device_id_type=MESH,
+            ).start()
+        )
 
     first = jnp.where(place == 0, 1.0, 0.0).astype(jnp.float32)
-    hand(0)
     for c in range(chunks):
-        if c + 1 < chunks:
-            hand(c + 1)
-        in_wait(c, 1)
+        @pl.when(place == 0)
+        def _():
+            in_wait(c, 1, 1, 6)
+            for k, plane in enumerate(z_sine(planes_of(c, 5))):
+                hhat[c, k * rows : (k + 1) * rows] = plane
+
+        @pl.when(place > 0)
+        def _():
+            in_wait(c, 1, 1, 5)
+            bulk(hhat.at[c], h_rs.at[c])
+
         fhat = [z_sine(planes_of(c, m + 1)) for m in range(4)]
         for m in range(4):
             for k in range(length_z):
                 part_b[c, m, k * rows : (k + 1) * rows] = fhat[m][k]
-
-        @pl.when(place == 0)
-        def _():
-            in_wait(c, 2)
-            for k, plane in enumerate(z_sine(planes_of(c, 5))):
-                hhat[c, k * rows : (k + 1) * rows] = plane
-
-        @pl.when(place > 0)
-        def _():
-            h_copy(c, after).wait_recv()
 
         def solve(i, carry):
             at = pl.ds(pl.multiple_of(i * block, 8), block)
@@ -486,104 +455,97 @@
             z_send[c, i, 1] = rest[4] + (gain + cross) * seen
             return carry
 
-        lax.fori_loop(0, owners, solve, 0, unroll=4)
+        lax.fori_loop(0, group, solve, 0, unroll=4)
         if c == 0:
             opened()
 
-        @pl.when(place < slices - 1)
-        def _():
-            peers(lambda peer: to_owner(peer, lambda: z_copy(c, peer, place).start()))
-
-        @pl.when(place < owners)
-        def _():
-            z_recv[c, place] = z_send[c, place]
-
-    peers(lambda peer: step_copy(peer, peer).wait_recv())
-
-    @pl.when(place < owners)
-    def _():
-        def one(p, carry):
-            for c in range(chunks):
-                at = pl.ds(pl.multiple_of(place * block, 8), block)
-                gains, crossed = gains_of(steps[p][0:1] * ell[c, at])
-                own_gain[c, p] = gains[4]
-                own_cross[c, p] = crossed[4]
-            return carry
-
-        lax.fori_loop(0, slices - 1, one, 0)
-
-    def r_copy(c, target, owner):
-        return pltpu.make_async_remote_copy(
-            src_ref=r_send.at[c, target],
-            dst_ref=r_recv.at[c, owner],
-            send_sem=r_ss.at[c],
+        pl.when(place < slices - 1)(lambda: z_start(c))
+        z_recv[c, mine] = z_send[c, mine]
+
+    bulk(steps.at[0 : group - 1], step_rs)
+    at = pl.ds(pl.multiple_of(mine * block, 8), block)
+
+    def one(p, carry):
+        for c in range(chunks):
+            gains, crossed = gains_of(steps[p][0:1] * ell[c, at])
+            own_gain[c, p] = gains[4]
+            own_cross[c, p] = crossed[4]
+        return carry
+
+    lax.fori_loop(0, group, one, 0)
+
+    def r_start(c, other):
+        pltpu.make_async_remote_copy(
+            src_ref=r_send.at[c, other],
+            dst_ref=r_recv.at[c, mine],
+            send_sem=r_ss,
             recv_sem=r_rs.at[c],
-            device_id={"tm": target},
+            device_id={"tm": eldest + other},
             device_id_type=MESH,
-        )
-
+        ).start()
+
+    short = jnp.logical_and(family == last_group, place < slices - 1)
     for c in range(chunks):
-        @pl.when(place < owners)
-        def _():
-            def scan(p, state):
-                @pl.when(p != place)
-                def _():
-                    z_copy(c, p, p).wait_recv()
-
-                lower, upper = state
-                gain = own_gain[c, p]
-                lower, upper = (
-                    gain * lower + z_recv[c, p, 0],
-                    gain * upper + own_cross[c, p] * lower + z_recv[c, p, 1],
-                )
-                target = p + 1
-                r_send[c, target, 0] = lower
-                r_send[c, target, 1] = upper
-
-                @pl.when(target != place)
-                def _():
-                    r_copy(c, target, place).start()
-
-                @pl.when(target == place)
-                def _():
-                    r_recv[c, place, 0] = lower
-                    r_recv[c, place, 1] = upper
-
-                return lower, upper
-
-            zero = jnp.zeros((block, width_y), jnp.float32)
-            state = (zero, zero)
-            if slices > UNROLL:
-                lax.fori_loop(0, slices - 1, scan, state)
-            else:
-                for p in range(slices - 1):
-                    state = scan(p, state)
+        if group > 2:
+            pl.when(short)(lambda: bulk(z_recv.at[c, 0 : group - 2], z_rs.at[c]))
+        pl.when(jnp.logical_not(short))(lambda: bulk(z_recv.at[c, 0 : group - 1], z_rs.at[c]))
+        pl.when(family > 0)(lambda: bulk(s_recv.at[c], s_rs.at[c]))
+
+        def advance(p, lower, upper):
+            gain = own_gain[c, p]
+            return (
+                gain * lower + z_recv[c, p, 0],
+                gain * upper + own_cross[c, p] * lower + z_recv[c, p, 1],
+            )
+
+        lower, upper = (jnp.where(family > 0, s_recv[c, i], 0.0) for i in range(2))
+        for p in range(group):
+            r_send[c, p, 0] = lower
+            r_send[c, p, 1] = upper
+            if p < group - 1:
+                lower, upper = advance(p, lower, upper)
+
+        @pl.when(family < last_group)
+        def _():
+            final = advance(group - 1, lower, upper)
+            s_send[c, 0], s_send[c, 1] = final
+            pltpu.make_async_remote_copy(
+                src_ref=s_send.at[c],
+                dst_ref=s_recv.at[c],
+                send_sem=s_ss,
+                recv_sem=s_rs.at[c],
+                device_id={"tm": place + group},
+                device_id_type=MESH,
+            ).start()
+
+        relatives(lambda other: pl.when(eldest + other > 0)(lambda: r_start(c, other)))
+        r_recv[c, mine] = r_send[c, mine]
+
+    halves = ((0, 3), (3, 5))
 
     def o_groups(c):
-        return tuple((m, m + 1) for m in range(5)) if c == chunks - 1 else ((0, 5),)
-
-    def o_copy(c, group, peer, source):
-        low, high = o_groups(c)[group]
-        return pltpu.make_async_remote_copy(
-            src_ref=o_send.at[c, peer, low:high],
-            dst_ref=o_recv.at[c, source, low:high],
-            send_sem=o_ss.at[c, group, peer],
-            recv_sem=o_rs.at[c, group, source],
-            device_id={"space": peer},
-            device_id_type=MESH,
-        )
-
-    def o_wait(c, group):
+        return halves if c == chunks - 1 else ((0, 5),)
+
+    def o_start(c, number):
+        low, high = o_groups(c)[number]
         for i in range(1, spaces):
             peer = lax.rem(me + i, spaces)
-            o_copy(c, group, peer, peer).wait_recv()
+            pltpu.make_async_remote_copy(
+                src_ref=o_send.at[c, peer, low:high],
+                dst_ref=o_recv.at[c, me, low:high],
+                send_sem=o_ss,
+                recv_sem=o_rs.at[c + number],
+                device_id={"space": peer},
+                device_id_type=MESH,
+            ).start()
+
+    def o_wait(c, number):
+        low, high = o_groups(c)[number]
+        bulk(o_recv.at[c, 0 : spaces - 1, low:high], o_rs.at[c + number])
 
     for c in range(chunks):
-        @pl.when(place > 0)
-        def _():
-            owner_wait(r_recv.at[c], r_rs.at[c])
-
-        own = hhat[c].reshape(owners, block, width_y)
+        pl.when(place > 0)(lambda: bulk(r_recv.at[c, 0 : group - 1], r_rs.at[c]))
+        own = hhat[c].reshape(group, block, width_y)
         lower = jnp.where(place == 0, own, r_recv[c, :, 0]).reshape(length_z * rows, width_y)
         upper = jnp.where(place == 0, own, r_recv[c, :, 1]).reshape(length_z * rows, width_y)
         for m in range(5):
@@ -596,10 +558,9 @@
             planes = z_sine([value[k * rows : (k + 1) * rows] for k in range(length_z)])
             for z in range(length_z):
                 o_send[c, z // depth, m, z % depth] = planes[z]
-            for group, (_, high) in enumerate(o_groups(c)):
+            for number, (_, high) in enumerate(o_groups(c)):
                 if high == m + 1:
-                    for i in range(1, spaces):
-                        o_copy(c, group, lax.rem(me + i, spaces), me).start()
+                    o_start(c, number)
             o_recv[c, me, m] = o_send[c, me, m]
 
     def unmix(c, low, high):
@@ -626,39 +587,30 @@
     for c in range(chunks - 1):
         o_wait(c, 0)
         unmix(c, 0, 5)
-    for m in range(5):
-        o_wait(chunks - 1, m)
-        unmix(chunks - 1, m, m + 1)
-        out = along_x(mix[m], mix[m, :width_x], x_ref, low_ref)
-        for z in range(depth):
-            result_ref[0, m, z] = out[:, z * width_y : (z + 1) * width_y]
-
-    for c in range(chunks):
-        for i in range(1, spaces):
-            peer = lax.rem(me + i, spaces)
-            in_copy(c, 0, peer, me).wait_send()
-            in_copy(c, 1, peer, me).wait_send()
-
-        @pl.when(place == 0)
-        def _():
-            for i in range(1, spaces):
-                in_copy(c, 2, lax.rem(me + i, spaces), me).wait_send()
-
-        @pl.when(place < slices - 1)
-        def _():
-            h_copy(c, after).wait_send()
-            owner_wait(z_send.at[c], z_ss.at[c])
-
-        @pl.when(place < owners)
-        def _():
-            pl.when(place == 0)(lambda: bulk_wait(r_send.at[c], r_ss.at[c], slices - 1))
-            pl.when(place > 0)(lambda: bulk_wait(r_send.at[c], r_ss.at[c], slices - 2))
-
-        for i in range(1, spaces):
-            for group in range(len(o_groups(c))):
-                o_copy(c, group, lax.rem(me + i, spaces), me).wait_send()
-
-    peers(lambda peer: step_copy(peer, place).wait_send())
+    for number, (low, high) in enumerate(halves):
+        o_wait(chunks - 1, number)
+        unmix(chunks - 1, low, high)
+        for m in range(low, high):
+            out = along_x(mix[m], mix[m, :width_x], x_ref, low_ref)
+            for z in range(depth):
+                result_ref[0, m, z] = out[:, z * width_y : (z + 1) * width_y]
+
+    others = spaces - 1
+    pl.when(place == 0)(lambda: bulk(in_send.at[:, 0:others], in_ss))
+    pl.when(place > 0)(lambda: bulk(in_send.at[:, 0:others, 0:5], in_ss))
+    bulk(o_send.at[:, 0:others], o_ss)
+    bulk(steps.at[0 : group - 1], step_ss)
+
+    @pl.when(place < slices - 1)
+    def _():
+        bulk(ghat, h_ss)
+        bulk(z_send.at[:, 0 : group - 1], z_ss)
+
+    pl.when(family < last_group)(lambda: bulk(s_send, s_ss))
+    fewer = jnp.logical_and(family == 0, place > 0)
+    if group > 2:
+        pl.when(fewer)(lambda: bulk(r_send.at[:, 0 : group - 2], r_ss))
+    pl.when(jnp.logical_not(fewer))(lambda: bulk(r_send.at[:, 0 : group - 1], r_ss))
 
 
 def body(initial, start_guess, forcing, step_size):
@@ -667,9 +619,9 @@
     length_z = depth * spaces
     chunks = CHUNKS
     rows = width_x // spaces // chunks
-    owners = min(slices, length_z * rows // 8)
-    block = length_z * rows // owners
-    dims = (spaces, slices, chunks, depth, length_z, rows, width_y, owners, block)
+    group = max(1, min(GROUP, slices // 2))
+    block = length_z * rows // group
+    dims = (spaces, slices, chunks, depth, length_z, rows, width_y, group, block)
 
     def pair(length):
         return split_pair(jnp.asarray(sine(length), jnp.float32))
@@ -688,7 +640,6 @@
     f32, b16 = jnp.float32, jnp.bfloat16
     flat = length_z * rows
     dma = pltpu.SemaphoreType.DMA
-    regular = pltpu.SemaphoreType.REGULAR
     vmem = pl.BlockSpec(memory_space=pltpu.VMEM)
     hbm = pl.BlockSpec(memory_space=pl.ANY)
     return pl.pallas_call(
@@ -710,35 +661,30 @@
             pltpu.VMEM((chunks, flat, width_y), f32),
             pltpu.VMEM((chunks, flat, width_y), f32),
             pltpu.VMEM((8, width_y), f32),
-            pltpu.VMEM((slices, 8, width_y), f32),
+            pltpu.VMEM((group, 8, width_y), f32),
             pltpu.VMEM((chunks, 4, flat, width_y), f32),
             pltpu.VMEM((chunks, 4, flat, width_y), f32),
             pltpu.VMEM((chunks, 4, flat, width_y), f32),
-            pltpu.VMEM((chunks, owners, 2, block, width_y), f32),
-            pltpu.VMEM((chunks, slices, 2, block, width_y), f32),
-            pltpu.VMEM((chunks, slices, block, width_y), f32),
-            pltpu.VMEM((chunks, slices, block, width_y), f32),
-            pltpu.VMEM((chunks, slices, 2, block, width_y), f32),
-            pltpu.VMEM((chunks, owners, 2, block, width_y), f32),
+            pltpu.VMEM((chunks, group, 2, block, width_y), f32),
+            pltpu.VMEM((chunks, group, 2, block, width_y), f32),
+            pltpu.VMEM((chunks, group, block, width_y), f32),
+            pltpu.VMEM((chunks, group, block, width_y), f32),
+            pltpu.VMEM((chunks, group, 2, block, width_y), f32),
+            pltpu.VMEM((chunks, group, 2, block, width_y), f32),
+            pltpu.VMEM((chunks, 2, block, width_y), f32),
+            pltpu.VMEM((chunks, 2, block, width_y), f32),
             pltpu.VMEM((chunks, spaces, 5, depth, rows, width_y), f32),
             pltpu.VMEM((chunks, spaces, 5, depth, rows, width_y), f32),
             pltpu.VMEM((5, 2 * width_x, depth * width_y), b16),
             dma((7,)),
-            dma((chunks, 3, spaces)),
-            dma((chunks, 3, spaces)),
+            dma((chunks, 2)),
             dma((chunks,)),
             dma((chunks,)),
-            dma((slices,)),
-            dma((slices,)),
-            dma((chunks,)),
-            dma((chunks, slices)),
             dma((chunks,)),
             dma((chunks,)),
-            dma((chunks, 5, spaces)),
-            dma((chunks, 5, spaces)),
-            regular,
-            regular,
-            regular,
+            dma((chunks + 1,)),
+            dma((8,)),
+            pltpu.SemaphoreType.REGULAR((3,)),
         ],
         compiler_params=pltpu.CompilerParams(collective_id=0, has_side_effects=True),
     )(step_size, initial, start_guess, forcing, x_twice, x_low, w, sides)

time: 36.9 us -> 29.3 us (0.79)
  the two profiles are of different devices: /device:TPU:0 before, /device:TPU:17 now
where the time goes in v2:
time: 29.3 us; the launch traced here: 29.1 us
  Pallas kernels  27.6 us (94%)
  local copies, waits for them, and re-layouts  0.84 us (3%)
  between operations  0.66 us (2%)
    pallas_call x1, Pallas kernels, body(): pl.pallas_call(functools.partial(kernel, dims), out_shape=pltpu.VMEM((1,...  27.6 us
    unnamed x1, local copies, waits for them, and re-layouts  0.84 us

profile of v2, /device:TPU:17, one launch (start us, length us, event | category | flops | bytes accessed | tf_op | source)
XLA Modules:
  0.0 29.1 jit_solution(13247673679033732073)
XLA Ops:
  0.7 27.6 %shard_map.73 = f32[1,5,2,128,128]{4,3,2,1,0:T(8,128)S(1)} custom-call(f32[1]{0:T(128)S(6)} %copy.10.step_ref, f32[2,128,128]{2,1,0:T(8,128)} %initial_hbm.1, f32[1,2,128,128]{3,2,1,0:T(8,128)} %guess_hbm.1, f32[1,5,2,128,128]{4,3,2,1,0:T(8,128)} %forcing_hbm.1, bf16[128,256]{1,0:T(8,128)(2,1)} %constant.15.x_hbm, bf16[128,128]{1,0:T(8,128)(2,1)} %constant.18.low_hbm, ...), custom_call_target="tpu_custom_call" | custom-call | tf_op jit(solution)/shard_map/pallas_call | solution.py:645
  28.3 0.8 %copy.9 = f32[1,5,2,128,128]{4,3,2,1,0:T(8,128)} copy(f32[1,5,2,128,128]{4,3,2,1,0:T(8,128)S(1)} %shard_map.73) | data formatting | bytes 1310720

commit v3 on v2

--- a/solution.py
+++ b/solution.py
@@ -196,7 +196,7 @@
     result_ref,
     initial, guess, forcing, x_ref, low_ref, w_ref, lateral_ref,
     in_send, in_recv, ghat, hhat, ell, own_step, steps,
-    gain_c, gain_d, part_b, z_send, z_recv, own_gain, own_cross, r_send, r_recv,
+    first_hat, gain_c, gain_d, part_b, z_send, z_recv, own_gain, own_cross, r_send, r_recv,
     s_send, s_recv, o_send, o_recv, mix,
     load_sem, in_rs, h_rs, z_rs, s_rs, r_rs, o_rs, sent, signals,
 ):
@@ -210,7 +210,10 @@
     family, mine = place // group, lax.rem(place, group)
     eldest = place - mine
     near_sem, next_sem, open_sem = (signals.at[i] for i in range(3))
-    in_ss, h_ss, step_ss, z_ss, s_ss, r_ss, o_ss, step_rs = (sent.at[i] for i in range(8))
+    h_ss, step_ss, z_ss, s_ss, r_ss, o_ss, step_rs = (sent.at[i] for i in range(7))
+    in_ss = [sent.at[7 + i] for i in range(4)]
+    first_in_ss, first_in_rs, first_ss = (sent.at[11 + i] for i in range(3))
+    helper = jnp.logical_and(family == 0, mine < chunks)
 
     barrier = pltpu.get_barrier_semaphore()
     odd = lax.rem(me, 2) == 1
@@ -255,20 +258,20 @@
     def keep(c, low, high):
         in_recv[c, me, low:high] = in_send[c, me, low:high]
 
-    def in_start(c, sem, low, high):
+    def in_start(c, low, high, left, landed):
         for i in range(1, spaces):
             peer = lax.rem(me + i, spaces)
             pltpu.make_async_remote_copy(
                 src_ref=in_send.at[c, peer, low:high],
                 dst_ref=in_recv.at[c, me, low:high],
-                send_sem=in_ss,
-                recv_sem=in_rs.at[c, sem],
+                send_sem=left,
+                recv_sem=landed,
                 device_id={"space": peer},
                 device_id_type=MESH,
             ).start()
 
-    def in_wait(c, sem, low, high):
-        bulk(in_recv.at[c, 0 : spaces - 1, low:high], in_rs.at[c, sem])
+    def in_wait(c, low, high, landed):
+        bulk(in_recv.at[c, 0 : spaces - 1, low:high], landed)
 
     load_guess.wait()
     load_w.wait()
@@ -285,12 +288,23 @@
     def _():
         pl.semaphore_wait(near_sem, 1)
 
-    for c in range(chunks):
-        in_start(c, 0, 0, 1)
-
-    @pl.when(jnp.logical_and(me == 0, place > 0))
-    def _():
-        pl.semaphore_signal(barrier, inc=1, device_id={"tm": place - 1}, device_id_type=MESH)
+    def guess_start(c):
+        in_start(c, 0, 1, in_ss[0], in_rs.at[c, 0])
+
+    for c in range(chunks // 2):
+        guess_start(c)
+
+    def greet(target):
+        pl.semaphore_signal(barrier, inc=1, device_id={"tm": target}, device_id_type=MESH)
+
+    @pl.when(me == 0)
+    def _():
+        pl.when(place > 0)(lambda: greet(place - 1))
+
+        @pl.when(place == 0)
+        def _():
+            for other in range(1, min(chunks, group)):
+                greet(other)
 
     def relatives(action):
         for i in range(1, group):
@@ -298,9 +312,6 @@
 
     @pl.when(me == everyone)
     def _():
-        def greet(target):
-            pl.semaphore_signal(barrier, inc=1, device_id={"tm": target}, device_id_type=MESH)
-
         relatives(lambda other: greet(eldest + other))
         pl.when(family > 0)(lambda: greet(place - group))
 
@@ -310,31 +321,34 @@
                 sem, inc=1, device_id={"space": lax.rem(me + i, spaces)}, device_id_type=MESH
             )
 
+    load_initial.wait()
+
+    @pl.when(helper)
+    def _():
+        put(initial[...], 5)
+        in_start(mine, 5, 6, first_in_ss, first_in_rs)
+        keep(mine, 5, 6)
+
+    for c in range(chunks // 2, chunks):
+        guess_start(c)
     for c in range(chunks):
         keep(c, 0, 1)
     load_forcing.wait()
     for m in range(4):
         put(step * weighted(integrals[m], [forcing[j] for j in range(5)]), m + 1)
 
-    load_initial.wait()
-
-    @pl.when(place == 0)
-    def _():
-        put(initial[...], 5)
-        for c in range(chunks):
-            in_start(c, 1, 1, 6)
-
-    @pl.when(place > 0)
-    def _():
-        for c in range(chunks):
-            in_start(c, 1, 1, 5)
+    last_left = 3
+
+    def forcing_start(c):
+        in_start(c, 1, 5, in_ss[min(c + 1, last_left)], in_rs.at[c, 1])
+
+    def forcing_left(c):
+        bulk(in_send.at[c, 0 : spaces - 1, 1:5], in_ss[c + 1])
+
+    forcing_start(0)
 
     for c in range(chunks):
         keep(c, 1, 5)
-
-        @pl.when(place == 0)
-        def _():
-            keep(c, 5, 6)
 
     z_eigen = eigen(length_z)
     load_lateral.wait()
@@ -358,55 +372,82 @@
     def planes_of(c, slot):
         return [in_recv[c, z // depth, slot, z % depth] for z in range(length_z)]
 
-    @pl.when(place < slices - 1)
-    def _():
-        @pl.when(me == 0)
-        def _():
-            pl.semaphore_wait(barrier, 1)
-            tell(next_sem)
-
-        @pl.when(me != 0)
-        def _():
-            pl.semaphore_wait(next_sem, 1)
-
+    helping = jnp.logical_and(helper, place > 0)
+    hands = jnp.logical_or(helping, place < slices - 1)
+
+    @pl.when(me == 0)
+    def _():
+        both = jnp.logical_and(helping, place < slices - 1)
+        pl.when(both)(lambda: pl.semaphore_wait(barrier, 2))
+        pl.when(jnp.logical_and(hands, jnp.logical_not(both)))(
+            lambda: pl.semaphore_wait(barrier, 1)
+        )
+        pl.when(hands)(lambda: tell(next_sem))
+
+    bulk(in_send.at[:, 0 : spaces - 1, 0:1], in_ss[0])
+    if chunks > 1:
+        forcing_start(1)
+
+    pl.when(jnp.logical_and(hands, me != 0))(lambda: pl.semaphore_wait(next_sem, 1))
     after = lax.rem(place + 1, slices)
-    for c in range(chunks):
-        in_wait(c, 0, 0, 1)
+    def hand(source, target, c, left):
+        pltpu.make_async_remote_copy(
+            src_ref=source,
+            dst_ref=hhat.at[c],
+            send_sem=left,
+            recv_sem=h_rs.at[c],
+            device_id={"tm": target},
+            device_id_type=MESH,
+        ).start()
+
+    def hand_guess(c):
+        in_wait(c, 0, 1, in_rs.at[c, 0])
         for k, plane in enumerate(z_sine(planes_of(c, 0))):
             ghat[c, k * rows : (k + 1) * rows] = plane
-
-        @pl.when(place < slices - 1)
+        pl.when(place < slices - 1)(lambda: hand(ghat.at[c], after, c, h_ss))
+
+    for c in range(chunks // 2):
+        hand_guess(c)
+
+    @pl.when(helper)
+    def _():
+        in_wait(mine, 5, 6, first_in_rs)
+        for k, plane in enumerate(z_sine(planes_of(mine, 5))):
+            first_hat[k * rows : (k + 1) * rows] = plane
+
+        @pl.when(place == 0)
         def _():
-            pltpu.make_async_remote_copy(
-                src_ref=ghat.at[c],
-                dst_ref=hhat.at[c],
-                send_sem=h_ss,
-                recv_sem=h_rs.at[c],
-                device_id={"tm": after},
-                device_id_type=MESH,
-            ).start()
-
-    def opened():
-        @pl.when(me == everyone)
-        def _():
-            pl.when(family < last_group)(lambda: pl.semaphore_wait(barrier, group))
-            pl.when(family == last_group)(lambda: pl.semaphore_wait(barrier, group - 1))
-            tell(open_sem)
-
-        @pl.when(me != everyone)
-        def _():
-            pl.semaphore_wait(open_sem, 1)
-
-        relatives(
-            lambda other: pltpu.make_async_remote_copy(
-                src_ref=own_step,
-                dst_ref=steps.at[mine],
-                send_sem=step_ss,
-                recv_sem=step_rs,
-                device_id={"tm": eldest + other},
-                device_id_type=MESH,
-            ).start()
-        )
+            hhat[0] = first_hat[...]
+
+        pl.when(place > 0)(lambda: hand(first_hat, 0, mine, first_ss))
+
+    for c in range(chunks // 2, chunks):
+        hand_guess(c)
+    for c in range(2, chunks):
+        if c < last_left + 1:
+            forcing_left(c - 2)
+        forcing_start(c)
+
+        if c == 2:
+            @pl.when(me == everyone)
+            def _():
+                pl.when(family < last_group)(lambda: pl.semaphore_wait(barrier, group))
+                pl.when(family == last_group)(lambda: pl.semaphore_wait(barrier, group - 1))
+                tell(open_sem)
+
+    pl.when(me != everyone)(lambda: pl.semaphore_wait(open_sem, 1))
+    relatives(
+        lambda other: pltpu.make_async_remote_copy(
+            src_ref=own_step,
+            dst_ref=steps.at[mine],
+            send_sem=step_ss,
+            recv_sem=step_rs,
+            device_id={"tm": eldest + other},
+            device_id_type=MESH,
+        ).start()
+    )
+
+    youngest = jnp.where(mine == group - 1, 1, 0)
 
     def z_start(c):
         relatives(
@@ -414,25 +455,20 @@
                 src_ref=z_send.at[c, other],
                 dst_ref=z_recv.at[c, mine],
                 send_sem=z_ss,
-                recv_sem=z_rs.at[c],
+                recv_sem=z_rs.at[c, youngest],
                 device_id={"tm": eldest + other},
                 device_id_type=MESH,
             ).start()
         )
 
     first = jnp.where(place == 0, 1.0, 0.0).astype(jnp.float32)
-    for c in range(chunks):
-        @pl.when(place == 0)
-        def _():
-            in_wait(c, 1, 1, 6)
-            for k, plane in enumerate(z_sine(planes_of(c, 5))):
-                hhat[c, k * rows : (k + 1) * rows] = plane
-
-        @pl.when(place > 0)
-        def _():
-            in_wait(c, 1, 1, 5)
+
+    def chunk(c):
+        in_wait(c, 1, 5, in_rs.at[c, 1])
+        if c == 0:
+            pl.when(place > 0)(lambda: bulk(hhat.at[c], h_rs.at[c]))
+        else:
             bulk(hhat.at[c], h_rs.at[c])
-
         fhat = [z_sine(planes_of(c, m + 1)) for m in range(4)]
         for m in range(4):
             for k in range(length_z):
@@ -456,23 +492,22 @@
             return carry
 
         lax.fori_loop(0, group, solve, 0, unroll=4)
-        if c == 0:
-            opened()
-
         pl.when(place < slices - 1)(lambda: z_start(c))
         z_recv[c, mine] = z_send[c, mine]
 
-    bulk(steps.at[0 : group - 1], step_rs)
     at = pl.ds(pl.multiple_of(mine * block, 8), block)
 
-    def one(p, carry):
-        for c in range(chunks):
-            gains, crossed = gains_of(steps[p][0:1] * ell[c, at])
-            own_gain[c, p] = gains[4]
-            own_cross[c, p] = crossed[4]
-        return carry
-
-    lax.fori_loop(0, group, one, 0)
+    def own_tables():
+        bulk(steps.at[0 : group - 1], step_rs)
+
+        def one(p, carry):
+            for c in range(chunks):
+                gains, crossed = gains_of(steps[p][0:1] * ell[c, at])
+                own_gain[c, p] = gains[4]
+                own_cross[c, p] = crossed[4]
+            return carry
+
+        lax.fori_loop(0, group, one, 0)
 
     def r_start(c, other):
         pltpu.make_async_remote_copy(
@@ -484,11 +519,13 @@
             device_id_type=MESH,
         ).start()
 
-    short = jnp.logical_and(family == last_group, place < slices - 1)
-    for c in range(chunks):
-        if group > 2:
-            pl.when(short)(lambda: bulk(z_recv.at[c, 0 : group - 2], z_rs.at[c]))
-        pl.when(jnp.logical_not(short))(lambda: bulk(z_recv.at[c, 0 : group - 1], z_rs.at[c]))
+    def scan(c):
+        @pl.when(mine < group - 1)
+        def _():
+            if group > 2:
+                bulk(z_recv.at[c, 0 : group - 2], z_rs.at[c, 0])
+
+        pl.when(mine == group - 1)(lambda: bulk(z_recv.at[c, 0 : group - 1], z_rs.at[c, 0]))
         pl.when(family > 0)(lambda: bulk(s_recv.at[c], s_rs.at[c]))
 
         def advance(p, lower, upper):
@@ -505,9 +542,13 @@
             if p < group - 1:
                 lower, upper = advance(p, lower, upper)
 
+        relatives(lambda other: pl.when(eldest + other > 0)(lambda: r_start(c, other)))
+        r_recv[c, mine] = r_send[c, mine]
+
         @pl.when(family < last_group)
         def _():
-            final = advance(group - 1, lower, upper)
+            pl.when(mine < group - 1)(lambda: bulk(z_recv.at[c, 0], z_rs.at[c, 1]))
+            final = advance(group - 1, r_send[c, group - 1, 0], r_send[c, group - 1, 1])
             s_send[c, 0], s_send[c, 1] = final
             pltpu.make_async_remote_copy(
                 src_ref=s_send.at[c],
@@ -517,9 +558,6 @@
                 device_id={"tm": place + group},
                 device_id_type=MESH,
             ).start()
-
-        relatives(lambda other: pl.when(eldest + other > 0)(lambda: r_start(c, other)))
-        r_recv[c, mine] = r_send[c, mine]
 
     halves = ((0, 3), (3, 5))
 
@@ -543,11 +581,7 @@
         low, high = o_groups(c)[number]
         bulk(o_recv.at[c, 0 : spaces - 1, low:high], o_rs.at[c + number])
 
-    for c in range(chunks):
-        pl.when(place > 0)(lambda: bulk(r_recv.at[c, 0 : group - 1], r_rs.at[c]))
-        own = hhat[c].reshape(group, block, width_y)
-        lower = jnp.where(place == 0, own, r_recv[c, :, 0]).reshape(length_z * rows, width_y)
-        upper = jnp.where(place == 0, own, r_recv[c, :, 1]).reshape(length_z * rows, width_y)
+    def give(c, lower, upper):
         for m in range(5):
             if m == 0:
                 value = upper
@@ -562,6 +596,37 @@
                 if high == m + 1:
                     o_start(c, number)
             o_recv[c, me, m] = o_send[c, me, m]
+
+    def give_first(c):
+        own = hhat[c]
+        give(c, own, own)
+
+    def give_later(c):
+        bulk(r_recv.at[c, 0 : group - 1], r_rs.at[c])
+        give(c, *(r_recv[c, :, i].reshape(length_z * rows, width_y) for i in range(2)))
+
+    for c in range(chunks - 1):
+        chunk(c)
+    own_tables()
+
+    @pl.when(place == 0)
+    def _():
+        scan(0)
+        chunk(chunks - 1)
+        for c in range(1, chunks):
+            scan(c)
+            give_first(c - 1)
+        give_first(chunks - 1)
+
+    @pl.when(place > 0)
+    def _():
+        chunk(chunks - 1)
+        for c in range(chunks):
+            scan(c)
+            if c >= 2:
+                give_later(c - 2)
+        for c in range(max(0, chunks - 2), chunks):
+            give_later(c)
 
     def unmix(c, low, high):
         stacked = jnp.concatenate(
@@ -596,8 +661,10 @@
                 result_ref[0, m, z] = out[:, z * width_y : (z + 1) * width_y]
 
     others = spaces - 1
-    pl.when(place == 0)(lambda: bulk(in_send.at[:, 0:others], in_ss))
-    pl.when(place > 0)(lambda: bulk(in_send.at[:, 0:others, 0:5], in_ss))
+    if chunks > 2:
+        bulk(in_send.at[2:chunks, 0:others, 1:5], in_ss[last_left])
+    pl.when(helper)(lambda: bulk(in_send.at[0, 0:others, 5:6], first_in_ss))
+    pl.when(helping)(lambda: bulk(first_hat, first_ss))
     bulk(o_send.at[:, 0:others], o_ss)
     bulk(steps.at[0 : group - 1], step_ss)
 
@@ -662,6 +729,7 @@
             pltpu.VMEM((chunks, flat, width_y), f32),
             pltpu.VMEM((8, width_y), f32),
             pltpu.VMEM((group, 8, width_y), f32),
+            pltpu.VMEM((flat, width_y), f32),
             pltpu.VMEM((chunks, 4, flat, width_y), f32),
             pltpu.VMEM((chunks, 4, flat, width_y), f32),
             pltpu.VMEM((chunks, 4, flat, width_y), f32),
@@ -679,11 +747,11 @@
             dma((7,)),
             dma((chunks, 2)),
             dma((chunks,)),
-            dma((chunks,)),
+            dma((chunks, 2)),
             dma((chunks,)),
             dma((chunks,)),
             dma((chunks + 1,)),
-            dma((8,)),
+            dma((14,)),
             pltpu.SemaphoreType.REGULAR((3,)),
         ],
         compiler_params=pltpu.CompilerParams(collective_id=0, has_side_effects=True),

time: 29.3 us -> 28.3 us (0.966)
  Pallas kernels: 27.6 us -> 26.7 us
    pallas_call x1, Pallas kernels: 27.6 us -> 26.7 us  [body(): pl.pallas_call(functools.partial(kernel, dims), out_shape=pltpu.VMEM((1,...]
where the time goes in v3:
time: 28.3 us; the launch traced here: 28.2 us
  Pallas kernels  26.7 us (94%)
  local copies, waits for them, and re-layouts  0.84 us (3%)
  between operations  0.66 us (2%)
    pallas_call x1, Pallas kernels, body(): pl.pallas_call(functools.partial(kernel, dims), out_shape=pltpu.VMEM((1,...  26.7 us
    unnamed x1, local copies, waits for them, and re-layouts  0.84 us

profile of v3, /device:TPU:17, one launch (start us, length us, event | category | flops | bytes accessed | tf_op | source)
XLA Modules:
  0.0 28.2 jit_solution(8875104120733606039)
XLA Ops:
  0.7 26.7 %shard_map.73 = f32[1,5,2,128,128]{4,3,2,1,0:T(8,128)S(1)} custom-call(f32[1]{0:T(128)S(6)} %copy.10.step_ref, f32[2,128,128]{2,1,0:T(8,128)} %initial_hbm.1, f32[1,2,128,128]{3,2,1,0:T(8,128)} %guess_hbm.1, f32[1,5,2,128,128]{4,3,2,1,0:T(8,128)} %forcing_hbm.1, bf16[128,256]{1,0:T(8,128)(2,1)} %constant.15.x_hbm, bf16[128,128]{1,0:T(8,128)(2,1)} %constant.18.low_hbm, ...), custom_call_target="tpu_custom_call" | custom-call | tf_op jit(solution)/shard_map/pallas_call | solution.py:712
  27.3 0.8 %copy.9 = f32[1,5,2,128,128]{4,3,2,1,0:T(8,128)} copy(f32[1,5,2,128,128]{4,3,2,1,0:T(8,128)S(1)} %shard_map.73) | data formatting | bytes 1310720

commit v4 on v3

--- a/solution.py
+++ b/solution.py
@@ -200,11 +200,13 @@
     s_send, s_recv, o_send, o_recv, mix,
     load_sem, in_rs, h_rs, z_rs, s_rs, r_rs, o_rs, sent, signals,
 ):
-    spaces, slices, chunks, depth, length_z, rows, width_y, group, block = dims
+    spaces, workers, slices, chunks, depth, length_z, rows, width_y, group, block = dims
     me = lax.axis_index("space")
     place = lax.axis_index("tm")
     _, integrals, _ = TABLES
-    width_x = spaces * chunks * rows
+    width_x = workers * chunks * rows
+    seat = me // 2
+    sub = 16 if block % 16 == 0 else 8
     everyone = spaces - 2
     last_group = slices // group - 1
     family, mine = place // group, lax.rem(place, group)
@@ -244,31 +246,38 @@
     def bulk(ref, sem):
         pltpu.make_async_copy(ref, ref, sem).wait()
 
-    def low_of(c, s):
-        return (c * spaces + s) * rows
+    def low_of(c, worker):
+        return (c * workers + worker) * rows
 
     def put(field, slot):
         planes = lateral(field, x_ref, low_ref, w_ref)
-        for target in range(spaces):
+        for target in range(workers):
             for c in range(chunks):
                 low = low_of(c, target)
                 for z in range(depth):
                     in_send[c, target, slot, z] = planes[z][low : low + rows]
 
     def keep(c, low, high):
-        in_recv[c, me, low:high] = in_send[c, me, low:high]
+        in_recv[c, me, low:high] = in_send[c, seat, low:high]
 
     def in_start(c, low, high, left, landed):
-        for i in range(1, spaces):
-            peer = lax.rem(me + i, spaces)
-            pltpu.make_async_remote_copy(
-                src_ref=in_send.at[c, peer, low:high],
-                dst_ref=in_recv.at[c, me, low:high],
-                send_sem=left,
-                recv_sem=landed,
-                device_id={"space": peer},
-                device_id_type=MESH,
-            ).start()
+        for worker in range(workers):
+            peer = 2 * worker + 1
+
+            @pl.when(me != peer)
+            def _():
+                pltpu.make_async_remote_copy(
+                    src_ref=in_send.at[c, worker, low:high],
+                    dst_ref=in_recv.at[c, me, low:high],
+                    send_sem=left,
+                    recv_sem=landed,
+                    device_id={"space": peer},
+                    device_id_type=MESH,
+                ).start()
+
+    def by_role(action):
+        pl.when(odd)(lambda: action(workers - 1))
+        pl.when(jnp.logical_not(odd))(lambda: action(workers))
 
     def in_wait(c, low, high, landed):
         bulk(in_recv.at[c, 0 : spaces - 1, low:high], landed)
@@ -316,9 +325,9 @@
         pl.when(family > 0)(lambda: greet(place - group))
 
     def tell(sem):
-        for i in range(1, spaces):
+        for worker in range(workers):
             pl.semaphore_signal(
-                sem, inc=1, device_id={"space": lax.rem(me + i, spaces)}, device_id_type=MESH
+                sem, inc=1, device_id={"space": 2 * worker + 1}, device_id_type=MESH
             )
 
     load_initial.wait()
@@ -327,12 +336,10 @@
     def _():
         put(initial[...], 5)
         in_start(mine, 5, 6, first_in_ss, first_in_rs)
-        keep(mine, 5, 6)
+        pl.when(odd)(lambda: keep(mine, 5, 6))
 
     for c in range(chunks // 2, chunks):
         guess_start(c)
-    for c in range(chunks):
-        keep(c, 0, 1)
     load_forcing.wait()
     for m in range(4):
         put(step * weighted(integrals[m], [forcing[j] for j in range(5)]), m + 1)
@@ -343,221 +350,39 @@
         in_start(c, 1, 5, in_ss[min(c + 1, last_left)], in_rs.at[c, 1])
 
     def forcing_left(c):
-        bulk(in_send.at[c, 0 : spaces - 1, 1:5], in_ss[c + 1])
+        by_role(lambda n: bulk(in_send.at[c, 0:n, 1:5], in_ss[c + 1]))
 
     forcing_start(0)
 
-    for c in range(chunks):
-        keep(c, 1, 5)
-
-    z_eigen = eigen(length_z)
-    load_lateral.wait()
-    for c in range(chunks):
-        low = pl.multiple_of(low_of(c, me), 8)
-        base = lateral_ref[pl.ds(low, rows), :]
-        for k in range(length_z):
-            ell[c, k * rows : (k + 1) * rows] = -(base + float(z_eigen[k]))
-
-    def table(i, carry):
-        for c in range(chunks):
-            at = pl.ds(pl.multiple_of(i * rows, 8), rows)
-            gains, crossed = gains_of(step * ell[c, at])
-            for m in range(1, 5):
-                gain_c[c, m - 1, at] = gains[m]
-                gain_d[c, m - 1, at] = crossed[m]
-        return carry
-
-    lax.fori_loop(0, length_z, table, 0)
-
-    def planes_of(c, slot):
-        return [in_recv[c, z // depth, slot, z % depth] for z in range(length_z)]
+    def guess_left():
+        by_role(lambda n: bulk(in_send.at[:, 0:n, 0:1], in_ss[0]))
 
     helping = jnp.logical_and(helper, place > 0)
     hands = jnp.logical_or(helping, place < slices - 1)
 
-    @pl.when(me == 0)
+    @pl.when(jnp.logical_not(odd))
     def _():
-        both = jnp.logical_and(helping, place < slices - 1)
-        pl.when(both)(lambda: pl.semaphore_wait(barrier, 2))
-        pl.when(jnp.logical_and(hands, jnp.logical_not(both)))(
-            lambda: pl.semaphore_wait(barrier, 1)
-        )
-        pl.when(hands)(lambda: tell(next_sem))
-
-    bulk(in_send.at[:, 0 : spaces - 1, 0:1], in_ss[0])
-    if chunks > 1:
-        forcing_start(1)
-
-    pl.when(jnp.logical_and(hands, me != 0))(lambda: pl.semaphore_wait(next_sem, 1))
-    after = lax.rem(place + 1, slices)
-    def hand(source, target, c, left):
-        pltpu.make_async_remote_copy(
-            src_ref=source,
-            dst_ref=hhat.at[c],
-            send_sem=left,
-            recv_sem=h_rs.at[c],
-            device_id={"tm": target},
-            device_id_type=MESH,
-        ).start()
-
-    def hand_guess(c):
-        in_wait(c, 0, 1, in_rs.at[c, 0])
-        for k, plane in enumerate(z_sine(planes_of(c, 0))):
-            ghat[c, k * rows : (k + 1) * rows] = plane
-        pl.when(place < slices - 1)(lambda: hand(ghat.at[c], after, c, h_ss))
-
-    for c in range(chunks // 2):
-        hand_guess(c)
-
-    @pl.when(helper)
-    def _():
-        in_wait(mine, 5, 6, first_in_rs)
-        for k, plane in enumerate(z_sine(planes_of(mine, 5))):
-            first_hat[k * rows : (k + 1) * rows] = plane
-
-        @pl.when(place == 0)
+        @pl.when(me == 0)
         def _():
-            hhat[0] = first_hat[...]
-
-        pl.when(place > 0)(lambda: hand(first_hat, 0, mine, first_ss))
-
-    for c in range(chunks // 2, chunks):
-        hand_guess(c)
-    for c in range(2, chunks):
-        if c < last_left + 1:
-            forcing_left(c - 2)
-        forcing_start(c)
-
-        if c == 2:
-            @pl.when(me == everyone)
-            def _():
-                pl.when(family < last_group)(lambda: pl.semaphore_wait(barrier, group))
-                pl.when(family == last_group)(lambda: pl.semaphore_wait(barrier, group - 1))
-                tell(open_sem)
-
-    pl.when(me != everyone)(lambda: pl.semaphore_wait(open_sem, 1))
-    relatives(
-        lambda other: pltpu.make_async_remote_copy(
-            src_ref=own_step,
-            dst_ref=steps.at[mine],
-            send_sem=step_ss,
-            recv_sem=step_rs,
-            device_id={"tm": eldest + other},
-            device_id_type=MESH,
-        ).start()
-    )
-
-    youngest = jnp.where(mine == group - 1, 1, 0)
-
-    def z_start(c):
-        relatives(
-            lambda other: pltpu.make_async_remote_copy(
-                src_ref=z_send.at[c, other],
-                dst_ref=z_recv.at[c, mine],
-                send_sem=z_ss,
-                recv_sem=z_rs.at[c, youngest],
-                device_id={"tm": eldest + other},
-                device_id_type=MESH,
-            ).start()
-        )
-
-    first = jnp.where(place == 0, 1.0, 0.0).astype(jnp.float32)
-
-    def chunk(c):
-        in_wait(c, 1, 5, in_rs.at[c, 1])
-        if c == 0:
-            pl.when(place > 0)(lambda: bulk(hhat.at[c], h_rs.at[c]))
-        else:
-            bulk(hhat.at[c], h_rs.at[c])
-        fhat = [z_sine(planes_of(c, m + 1)) for m in range(4)]
-        for m in range(4):
-            for k in range(length_z):
-                part_b[c, m, k * rows : (k + 1) * rows] = fhat[m][k]
-
-        def solve(i, carry):
-            at = pl.ds(pl.multiple_of(i * block, 8), block)
-            rate = step * ell[c, at]
-            middle = 1.0 + 0.5 * rate
-            guess_hat, start = ghat[c, at], hhat[c, at]
-            sources = [part_b[c, m, at] for m in range(4)]
-            one = sweep(rate, [start] + [guess_hat] * 4, sources)
-            nodes = corrected(*one, middle)
-            rest = corrected(*sweep(rate, nodes, sources), middle)
-            for m in range(1, 5):
-                part_b[c, m - 1, at] = rest[m]
-            seen = first * start
-            gain, cross = gain_c[c, 3, at], gain_d[c, 3, at]
-            z_send[c, i, 0] = nodes[4] + gain * seen
-            z_send[c, i, 1] = rest[4] + (gain + cross) * seen
-            return carry
-
-        lax.fori_loop(0, group, solve, 0, unroll=4)
-        pl.when(place < slices - 1)(lambda: z_start(c))
-        z_recv[c, mine] = z_send[c, mine]
-
-    at = pl.ds(pl.multiple_of(mine * block, 8), block)
-
-    def own_tables():
-        bulk(steps.at[0 : group - 1], step_rs)
-
-        def one(p, carry):
-            for c in range(chunks):
-                gains, crossed = gains_of(steps[p][0:1] * ell[c, at])
-                own_gain[c, p] = gains[4]
-                own_cross[c, p] = crossed[4]
-            return carry
-
-        lax.fori_loop(0, group, one, 0)
-
-    def r_start(c, other):
-        pltpu.make_async_remote_copy(
-            src_ref=r_send.at[c, other],
-            dst_ref=r_recv.at[c, mine],
-            send_sem=r_ss,
-            recv_sem=r_rs.at[c],
-            device_id={"tm": eldest + other},
-            device_id_type=MESH,
-        ).start()
-
-    def scan(c):
-        @pl.when(mine < group - 1)
-        def _():
-            if group > 2:
-                bulk(z_recv.at[c, 0 : group - 2], z_rs.at[c, 0])
-
-        pl.when(mine == group - 1)(lambda: bulk(z_recv.at[c, 0 : group - 1], z_rs.at[c, 0]))
-        pl.when(family > 0)(lambda: bulk(s_recv.at[c], s_rs.at[c]))
-
-        def advance(p, lower, upper):
-            gain = own_gain[c, p]
-            return (
-                gain * lower + z_recv[c, p, 0],
-                gain * upper + own_cross[c, p] * lower + z_recv[c, p, 1],
+            both = jnp.logical_and(helping, place < slices - 1)
+            pl.when(both)(lambda: pl.semaphore_wait(barrier, 2))
+            pl.when(jnp.logical_and(hands, jnp.logical_not(both)))(
+                lambda: pl.semaphore_wait(barrier, 1)
             )
-
-        lower, upper = (jnp.where(family > 0, s_recv[c, i], 0.0) for i in range(2))
-        for p in range(group):
-            r_send[c, p, 0] = lower
-            r_send[c, p, 1] = upper
-            if p < group - 1:
-                lower, upper = advance(p, lower, upper)
-
-        relatives(lambda other: pl.when(eldest + other > 0)(lambda: r_start(c, other)))
-        r_recv[c, mine] = r_send[c, mine]
-
-        @pl.when(family < last_group)
-        def _():
-            pl.when(mine < group - 1)(lambda: bulk(z_recv.at[c, 0], z_rs.at[c, 1]))
-            final = advance(group - 1, r_send[c, group - 1, 0], r_send[c, group - 1, 1])
-            s_send[c, 0], s_send[c, 1] = final
-            pltpu.make_async_remote_copy(
-                src_ref=s_send.at[c],
-                dst_ref=s_recv.at[c],
-                send_sem=s_ss,
-                recv_sem=s_rs.at[c],
-                device_id={"tm": place + group},
-                device_id_type=MESH,
-            ).start()
+            pl.when(hands)(lambda: tell(next_sem))
+
+        guess_left()
+        for c in range(1, chunks):
+            if 1 < c < last_left + 1:
+                forcing_left(c - 2)
+            forcing_start(c)
+
+            if c == 2:
+                @pl.when(me == everyone)
+                def _():
+                    pl.when(family < last_group)(lambda: pl.semaphore_wait(barrier, group))
+                    pl.when(family == last_group)(lambda: pl.semaphore_wait(barrier, group - 1))
+                    tell(open_sem)
 
     halves = ((0, 3), (3, 5))
 
@@ -570,7 +395,7 @@
             peer = lax.rem(me + i, spaces)
             pltpu.make_async_remote_copy(
                 src_ref=o_send.at[c, peer, low:high],
-                dst_ref=o_recv.at[c, me, low:high],
+                dst_ref=o_recv.at[c, seat, low:high],
                 send_sem=o_ss,
                 recv_sem=o_rs.at[c + number],
                 device_id={"space": peer},
@@ -579,54 +404,262 @@
 
     def o_wait(c, number):
         low, high = o_groups(c)[number]
-        bulk(o_recv.at[c, 0 : spaces - 1, low:high], o_rs.at[c + number])
-
-    def give(c, lower, upper):
-        for m in range(5):
-            if m == 0:
-                value = upper
+        by_role(lambda n: bulk(o_recv.at[c, 0:n, low:high], o_rs.at[c + number]))
+
+    load_lateral.wait()
+
+    @pl.when(odd)
+    def _():
+        for c in range(chunks):
+            keep(c, 0, 5)
+
+        z_eigen = eigen(length_z)
+        for c in range(chunks):
+            low = pl.multiple_of(low_of(c, seat), 8)
+            base = lateral_ref[pl.ds(low, rows), :]
+            for k in range(length_z):
+                ell[c, k * rows : (k + 1) * rows] = -(base + float(z_eigen[k]))
+
+        def table(i, carry):
+            for c in range(chunks):
+                at = pl.ds(pl.multiple_of(i * rows, 8), rows)
+                gains, crossed = gains_of(step * ell[c, at])
+                for m in range(1, 5):
+                    gain_c[c, m - 1, at] = gains[m]
+                    gain_d[c, m - 1, at] = crossed[m]
+            return carry
+
+        lax.fori_loop(0, length_z, table, 0)
+
+        def planes_of(c, slot):
+            return [in_recv[c, z // depth, slot, z % depth] for z in range(length_z)]
+
+        guess_left()
+        if chunks > 1:
+            forcing_start(1)
+
+        pl.when(hands)(lambda: pl.semaphore_wait(next_sem, 1))
+        after = lax.rem(place + 1, slices)
+
+        def hand(source, target, c, left):
+            pltpu.make_async_remote_copy(
+                src_ref=source,
+                dst_ref=hhat.at[c],
+                send_sem=left,
+                recv_sem=h_rs.at[c],
+                device_id={"tm": target},
+                device_id_type=MESH,
+            ).start()
+
+        def hand_guess(c):
+            in_wait(c, 0, 1, in_rs.at[c, 0])
+            for k, plane in enumerate(z_sine(planes_of(c, 0))):
+                ghat[c, k * rows : (k + 1) * rows] = plane
+            pl.when(place < slices - 1)(lambda: hand(ghat.at[c], after, c, h_ss))
+
+        for c in range(chunks // 2):
+            hand_guess(c)
+
+        @pl.when(helper)
+        def _():
+            in_wait(mine, 5, 6, first_in_rs)
+            for k, plane in enumerate(z_sine(planes_of(mine, 5))):
+                first_hat[k * rows : (k + 1) * rows] = plane
+
+            @pl.when(place == 0)
+            def _():
+                hhat[0] = first_hat[...]
+
+            pl.when(place > 0)(lambda: hand(first_hat, 0, mine, first_ss))
+
+        def forcing_next(c):
+            if c < chunks:
+                if c < last_left + 1:
+                    forcing_left(c - 2)
+                forcing_start(c)
+
+        forcing_next(2)
+        for c in range(chunks // 2, chunks):
+            hand_guess(c)
+        for c in range(3, chunks):
+            forcing_next(c)
+
+        pl.semaphore_wait(open_sem, 1)
+        relatives(
+            lambda other: pltpu.make_async_remote_copy(
+                src_ref=own_step,
+                dst_ref=steps.at[mine],
+                send_sem=step_ss,
+                recv_sem=step_rs,
+                device_id={"tm": eldest + other},
+                device_id_type=MESH,
+            ).start()
+        )
+
+        youngest = jnp.where(mine == group - 1, 1, 0)
+
+        def z_start(c):
+            relatives(
+                lambda other: pltpu.make_async_remote_copy(
+                    src_ref=z_send.at[c, other],
+                    dst_ref=z_recv.at[c, mine],
+                    send_sem=z_ss,
+                    recv_sem=z_rs.at[c, youngest],
+                    device_id={"tm": eldest + other},
+                    device_id_type=MESH,
+                ).start()
+            )
+
+        first = jnp.where(place == 0, 1.0, 0.0).astype(jnp.float32)
+
+        def chunk(c):
+            in_wait(c, 1, 5, in_rs.at[c, 1])
+            if c == 0:
+                pl.when(place > 0)(lambda: bulk(hhat.at[c], h_rs.at[c]))
             else:
-                value = (
-                    gain_c[c, m - 1] * upper + gain_d[c, m - 1] * lower + part_b[c, m - 1]
+                bulk(hhat.at[c], h_rs.at[c])
+            fhat = [z_sine(planes_of(c, m + 1)) for m in range(4)]
+            for m in range(4):
+                for k in range(length_z):
+                    part_b[c, m, k * rows : (k + 1) * rows] = fhat[m][k]
+
+            def solve(i, carry):
+                for part in range(block // sub):
+                    at = pl.ds(pl.multiple_of(i * block + part * sub, 8), sub)
+                    here = pl.ds(part * sub, sub)
+                    rate = step * ell[c, at]
+                    middle = 1.0 + 0.5 * rate
+                    guess_hat, start = ghat[c, at], hhat[c, at]
+                    sources = [part_b[c, m, at] for m in range(4)]
+                    one = sweep(rate, [start] + [guess_hat] * 4, sources)
+                    nodes = corrected(*one, middle)
+                    rest = corrected(*sweep(rate, nodes, sources), middle)
+                    for m in range(1, 5):
+                        part_b[c, m - 1, at] = rest[m]
+                    seen = first * start
+                    gain, cross = gain_c[c, 3, at], gain_d[c, 3, at]
+                    z_send[c, i, 0, here] = nodes[4] + gain * seen
+                    z_send[c, i, 1, here] = rest[4] + (gain + cross) * seen
+                return carry
+
+            lax.fori_loop(0, group, solve, 0, unroll=2)
+            pl.when(place < slices - 1)(lambda: z_start(c))
+            z_recv[c, mine] = z_send[c, mine]
+
+        def own_tables(c):
+            def one(p, carry):
+                for part in range(block // sub):
+                    at = pl.ds(pl.multiple_of(mine * block + part * sub, 8), sub)
+                    here = pl.ds(part * sub, sub)
+                    gains, crossed = gains_of(steps[p][0:1] * ell[c, at])
+                    own_gain[c, p, here] = gains[4]
+                    own_cross[c, p, here] = crossed[4]
+                return carry
+
+            lax.fori_loop(0, group, one, 0)
+
+        def r_start(c, other):
+            pltpu.make_async_remote_copy(
+                src_ref=r_send.at[c, other],
+                dst_ref=r_recv.at[c, mine],
+                send_sem=r_ss,
+                recv_sem=r_rs.at[c],
+                device_id={"tm": eldest + other},
+                device_id_type=MESH,
+            ).start()
+
+        def scan(c):
+            if c == 0:
+                bulk(steps.at[0 : group - 1], step_rs)
+            own_tables(c)
+
+            @pl.when(mine < group - 1)
+            def _():
+                if group > 2:
+                    bulk(z_recv.at[c, 0 : group - 2], z_rs.at[c, 0])
+
+            pl.when(mine == group - 1)(lambda: bulk(z_recv.at[c, 0 : group - 1], z_rs.at[c, 0]))
+            pl.when(family > 0)(lambda: bulk(s_recv.at[c], s_rs.at[c]))
+
+            def advance(p, lower, upper):
+                gain = own_gain[c, p]
+                return (
+                    gain * lower + z_recv[c, p, 0],
+                    gain * upper + own_cross[c, p] * lower + z_recv[c, p, 1],
                 )
-            planes = z_sine([value[k * rows : (k + 1) * rows] for k in range(length_z)])
-            for z in range(length_z):
-                o_send[c, z // depth, m, z % depth] = planes[z]
-            for number, (_, high) in enumerate(o_groups(c)):
-                if high == m + 1:
-                    o_start(c, number)
-            o_recv[c, me, m] = o_send[c, me, m]
-
-    def give_first(c):
-        own = hhat[c]
-        give(c, own, own)
-
-    def give_later(c):
-        bulk(r_recv.at[c, 0 : group - 1], r_rs.at[c])
-        give(c, *(r_recv[c, :, i].reshape(length_z * rows, width_y) for i in range(2)))
-
-    for c in range(chunks - 1):
-        chunk(c)
-    own_tables()
-
-    @pl.when(place == 0)
-    def _():
-        scan(0)
-        chunk(chunks - 1)
-        for c in range(1, chunks):
-            scan(c)
-            give_first(c - 1)
-        give_first(chunks - 1)
-
-    @pl.when(place > 0)
-    def _():
-        chunk(chunks - 1)
+
+            lower, upper = (jnp.where(family > 0, s_recv[c, i], 0.0) for i in range(2))
+            for p in range(group):
+                r_send[c, p, 0] = lower
+                r_send[c, p, 1] = upper
+                if p < group - 1:
+                    lower, upper = advance(p, lower, upper)
+
+            @pl.when(family < last_group)
+            def _():
+                pl.when(mine < group - 1)(lambda: bulk(z_recv.at[c, 0], z_rs.at[c, 1]))
+                final = advance(group - 1, r_send[c, group - 1, 0], r_send[c, group - 1, 1])
+                s_send[c, 0], s_send[c, 1] = final
+                pltpu.make_async_remote_copy(
+                    src_ref=s_send.at[c],
+                    dst_ref=s_recv.at[c],
+                    send_sem=s_ss,
+                    recv_sem=s_rs.at[c],
+                    device_id={"tm": place + group},
+                    device_id_type=MESH,
+                ).start()
+
+            relatives(lambda other: pl.when(eldest + other > 0)(lambda: r_start(c, other)))
+            r_recv[c, mine] = r_send[c, mine]
+
+        def give(c, lower, upper):
+            for m in range(5):
+                if m == 0:
+                    value = upper
+                else:
+                    value = (
+                        gain_c[c, m - 1] * upper + gain_d[c, m - 1] * lower + part_b[c, m - 1]
+                    )
+                planes = z_sine([value[k * rows : (k + 1) * rows] for k in range(length_z)])
+                for z in range(length_z):
+                    o_send[c, z // depth, m, z % depth] = planes[z]
+                for number, (_, high) in enumerate(o_groups(c)):
+                    if high == m + 1:
+                        o_start(c, number)
+                o_recv[c, seat, m] = o_send[c, me, m]
+
+        def give_first(c):
+            own = hhat[c]
+            give(c, own, own)
+
+        def give_later(c):
+            bulk(r_recv.at[c, 0 : group - 1], r_rs.at[c])
+            give(c, *(r_recv[c, :, i].reshape(length_z * rows, width_y) for i in range(2)))
+
+        early = max(0, chunks - 3)
         for c in range(chunks):
-            scan(c)
-            if c >= 2:
-                give_later(c - 2)
-        for c in range(max(0, chunks - 2), chunks):
-            give_later(c)
+            chunk(c)
+            if c == early:
+                pl.when(place == group - 1)(lambda: scan(0))
+            if c == max(0, chunks - 2):
+                pl.when(place < group - 1)(lambda: scan(0))
+        pl.when(family > 0)(lambda: scan(0))
+
+        @pl.when(place == 0)
+        def _():
+            for c in range(1, chunks):
+                scan(c)
+                give_first(c - 1)
+            give_first(chunks - 1)
+
+        @pl.when(place > 0)
+        def _():
+            for c in range(1, chunks):
+                scan(c)
+                if c >= 2:
+                    give_later(c - 2)
+            for c in range(max(0, chunks - 2), chunks):
+                give_later(c)
 
     def unmix(c, low, high):
         stacked = jnp.concatenate(
@@ -634,11 +667,11 @@
                 o_recv[c, s, m, z]
                 for m in range(low, high)
                 for z in range(depth)
-                for s in range(spaces)
+                for s in range(workers)
             ],
             axis=0,
         )
-        tall = spaces * rows
+        tall = workers * rows
         mixed_high, mixed_low = split_pair(along_y(stacked, w_ref))
         for m in range(low, high):
             for z in range(depth):
@@ -660,24 +693,26 @@
             for z in range(depth):
                 result_ref[0, m, z] = out[:, z * width_y : (z + 1) * width_y]
 
-    others = spaces - 1
     if chunks > 2:
-        bulk(in_send.at[2:chunks, 0:others, 1:5], in_ss[last_left])
-    pl.when(helper)(lambda: bulk(in_send.at[0, 0:others, 5:6], first_in_ss))
-    pl.when(helping)(lambda: bulk(first_hat, first_ss))
-    bulk(o_send.at[:, 0:others], o_ss)
-    bulk(steps.at[0 : group - 1], step_ss)
-
-    @pl.when(place < slices - 1)
+        by_role(lambda n: bulk(in_send.at[2:chunks, 0:n, 1:5], in_ss[last_left]))
+    pl.when(helper)(lambda: by_role(lambda n: bulk(in_send.at[0, 0:n, 5:6], first_in_ss)))
+
+    @pl.when(odd)
     def _():
-        bulk(ghat, h_ss)
-        bulk(z_send.at[:, 0 : group - 1], z_ss)
-
-    pl.when(family < last_group)(lambda: bulk(s_send, s_ss))
-    fewer = jnp.logical_and(family == 0, place > 0)
-    if group > 2:
-        pl.when(fewer)(lambda: bulk(r_send.at[:, 0 : group - 2], r_ss))
-    pl.when(jnp.logical_not(fewer))(lambda: bulk(r_send.at[:, 0 : group - 1], r_ss))
+        pl.when(helping)(lambda: bulk(first_hat, first_ss))
+        bulk(o_send.at[:, 0 : spaces - 1], o_ss)
+        bulk(steps.at[0 : group - 1], step_ss)
+
+        @pl.when(place < slices - 1)
+        def _():
+            bulk(ghat, h_ss)
+            bulk(z_send.at[:, 0 : group - 1], z_ss)
+
+        pl.when(family < last_group)(lambda: bulk(s_send, s_ss))
+        fewer = jnp.logical_and(family == 0, place > 0)
+        if group > 2:
+            pl.when(fewer)(lambda: bulk(r_send.at[:, 0 : group - 2], r_ss))
+        pl.when(jnp.logical_not(fewer))(lambda: bulk(r_send.at[:, 0 : group - 1], r_ss))
 
 
 def body(initial, start_guess, forcing, step_size):
@@ -685,10 +720,11 @@
     spaces, slices = lax.axis_size("space"), lax.axis_size("tm")
     length_z = depth * spaces
     chunks = CHUNKS
-    rows = width_x // spaces // chunks
+    workers = spaces // 2
+    rows = width_x // workers // chunks
     group = max(1, min(GROUP, slices // 2))
     block = length_z * rows // group
-    dims = (spaces, slices, chunks, depth, length_z, rows, width_y, group, block)
+    dims = (spaces, workers, slices, chunks, depth, length_z, rows, width_y, group, block)
 
     def pair(length):
         return split_pair(jnp.asarray(sine(length), jnp.float32))
@@ -722,7 +758,7 @@
             pltpu.VMEM((width_x, width_x), b16),
             pltpu.VMEM((2 * width_y, 2 * width_y), b16),
             pltpu.VMEM((width_x, width_y), f32),
-            pltpu.VMEM((chunks, spaces, 6, depth, rows, width_y), f32),
+            pltpu.VMEM((chunks, workers, 6, depth, rows, width_y), f32),
             pltpu.VMEM((chunks, spaces, 6, depth, rows, width_y), f32),
             pltpu.VMEM((chunks, flat, width_y), f32),
             pltpu.VMEM((chunks, flat, width_y), f32),
@@ -742,7 +778,7 @@
             pltpu.VMEM((chunks, 2, block, width_y), f32),
             pltpu.VMEM((chunks, 2, block, width_y), f32),
             pltpu.VMEM((chunks, spaces, 5, depth, rows, width_y), f32),
-            pltpu.VMEM((chunks, spaces, 5, depth, rows, width_y), f32),
+            pltpu.VMEM((chunks, workers, 5, depth, rows, width_y), f32),
             pltpu.VMEM((5, 2 * width_x, depth * width_y), b16),
             dma((7,)),
             dma((chunks, 2)),

time: 28.3 us -> 27.1 us (0.958)
  Pallas kernels: 26.7 us -> 25.4 us
    pallas_call x1, Pallas kernels: 26.7 us -> 25.4 us  [body(): pl.pallas_call(functools.partial(kernel, dims), out_shape=pltpu.VMEM((1,...]
where the time goes in v4:
time: 27.1 us; the launch traced here: 26.9 us
  Pallas kernels  25.4 us (94%)
  local copies, waits for them, and re-layouts  0.84 us (3%)
  between operations  0.66 us (2%)
    pallas_call x1, Pallas kernels, body(): pl.pallas_call(functools.partial(kernel, dims), out_shape=pltpu.VMEM((1,...  25.4 us
    unnamed x1, local copies, waits for them, and re-layouts  0.84 us

profile of v4, /device:TPU:17, one launch (start us, length us, event | category | flops | bytes accessed | tf_op | source)
XLA Modules:
  0.0 26.9 jit_solution(5945723906388084100)
XLA Ops:
  0.7 25.4 %shard_map.73 = f32[1,5,2,128,128]{4,3,2,1,0:T(8,128)S(1)} custom-call(f32[1]{0:T(128)S(6)} %copy.10.step_ref, f32[2,128,128]{2,1,0:T(8,128)} %initial_hbm.1, f32[1,2,128,128]{3,2,1,0:T(8,128)} %guess_hbm.1, f32[1,5,2,128,128]{4,3,2,1,0:T(8,128)} %forcing_hbm.1, bf16[128,256]{1,0:T(8,128)(2,1)} %constant.15.x_hbm, bf16[128,128]{1,0:T(8,128)(2,1)} %constant.18.low_hbm, ...), custom_call_target="tpu_custom_call" | custom-call | tf_op jit(solution)/shard_map/pallas_call | solution.py:748
  26.1 0.8 %copy.9 = f32[1,5,2,128,128]{4,3,2,1,0:T(8,128)} copy(f32[1,5,2,128,128]{4,3,2,1,0:T(8,128)S(1)} %shard_map.73) | data formatting | bytes 1310720

commit v5 on v4

--- a/solution.py
+++ b/solution.py
@@ -498,17 +498,15 @@
 
         youngest = jnp.where(mine == group - 1, 1, 0)
 
-        def z_start(c):
-            relatives(
-                lambda other: pltpu.make_async_remote_copy(
-                    src_ref=z_send.at[c, other],
-                    dst_ref=z_recv.at[c, mine],
-                    send_sem=z_ss,
-                    recv_sem=z_rs.at[c, youngest],
-                    device_id={"tm": eldest + other},
-                    device_id_type=MESH,
-                ).start()
-            )
+        def z_start(c, other):
+            pltpu.make_async_remote_copy(
+                src_ref=z_send.at[c, other],
+                dst_ref=z_recv.at[c, mine],
+                send_sem=z_ss,
+                recv_sem=z_rs.at[c, youngest],
+                device_id={"tm": eldest + other},
+                device_id_type=MESH,
+            ).start()
 
         first = jnp.where(place == 0, 1.0, 0.0).astype(jnp.float32)
 
@@ -542,8 +540,12 @@
                     z_send[c, i, 1, here] = rest[4] + (gain + cross) * seen
                 return carry
 
-            lax.fori_loop(0, group, solve, 0, unroll=2)
-            pl.when(place < slices - 1)(lambda: z_start(c))
+            half = group // 2
+            for i in [half] + [k for k in range(1, group) if k != half]:
+                other = lax.rem(mine + i, group)
+                solve(other, 0)
+                pl.when(place < slices - 1)(lambda: z_start(c, other))
+            solve(mine, 0)
             z_recv[c, mine] = z_send[c, mine]
 
         def own_tables(c):
@@ -652,14 +654,17 @@
                 give_first(c - 1)
             give_first(chunks - 1)
 
-        @pl.when(place > 0)
-        def _():
+        def later(lag):
             for c in range(1, chunks):
                 scan(c)
-                if c >= 2:
-                    give_later(c - 2)
-            for c in range(max(0, chunks - 2), chunks):
+                if c >= lag:
+                    give_later(c - lag)
+            for c in range(max(0, chunks - lag), chunks):
                 give_later(c)
+
+        soon = jnp.logical_and(family > 0, mine < group // 2)
+        pl.when(soon)(lambda: later(1))
+        pl.when(jnp.logical_and(place > 0, jnp.logical_not(soon)))(lambda: later(2))
 
     def unmix(c, low, high):
         stacked = jnp.concatenate(

time: 27.1 us -> 26.6 us (0.982)
  Pallas kernels: 25.4 us -> 25 us
    pallas_call x1, Pallas kernels: 25.4 us -> 25 us  [body(): pl.pallas_call(functools.partial(kernel, dims), out_shape=pltpu.VMEM((1,...]
where the time goes in v5:
time: 26.6 us; the launch traced here: 26.5 us
  Pallas kernels  25 us (94%)
  local copies, waits for them, and re-layouts  0.84 us (3%)
  between operations  0.66 us (2%)
    pallas_call x1, Pallas kernels, body(): pl.pallas_call(functools.partial(kernel, dims), out_shape=pltpu.VMEM((1,...  25 us
    unnamed x1, local copies, waits for them, and re-layouts  0.84 us

profile of v5, /device:TPU:17, one launch (start us, length us, event | category | flops | bytes accessed | tf_op | source)
XLA Modules:
  0.0 26.5 jit_solution(10538977717570047443)
XLA Ops:
  0.7 25.0 %shard_map.73 = f32[1,5,2,128,128]{4,3,2,1,0:T(8,128)S(1)} custom-call(f32[1]{0:T(128)S(6)} %copy.10.step_ref, f32[2,128,128]{2,1,0:T(8,128)} %initial_hbm.1, f32[1,2,128,128]{3,2,1,0:T(8,128)} %guess_hbm.1, f32[1,5,2,128,128]{4,3,2,1,0:T(8,128)} %forcing_hbm.1, bf16[128,256]{1,0:T(8,128)(2,1)} %constant.15.x_hbm, bf16[128,128]{1,0:T(8,128)(2,1)} %constant.18.low_hbm, ...), custom_call_target="tpu_custom_call" | custom-call | tf_op jit(solution)/shard_map/pallas_call | solution.py:753
  25.6 0.8 %copy.9 = f32[1,5,2,128,128]{4,3,2,1,0:T(8,128)} copy(f32[1,5,2,128,128]{4,3,2,1,0:T(8,128)S(1)} %shard_map.73) | data formatting | bytes 1310720

commit v6 on v5

--- a/solution.py
+++ b/solution.py
@@ -623,6 +623,9 @@
                         gain_c[c, m - 1] * upper + gain_d[c, m - 1] * lower + part_b[c, m - 1]
                     )
                 planes = z_sine([value[k * rows : (k + 1) * rows] for k in range(length_z)])
+                if c == chunks - 1:
+                    tall = along_y(jnp.concatenate(planes, axis=0), w_ref)
+                    planes = [tall[z * rows : (z + 1) * rows] for z in range(length_z)]
                 for z in range(length_z):
                     o_send[c, z // depth, m, z % depth] = planes[z]
                 for number, (_, high) in enumerate(o_groups(c)):
@@ -677,7 +680,8 @@
             axis=0,
         )
         tall = workers * rows
-        mixed_high, mixed_low = split_pair(along_y(stacked, w_ref))
+        mixed = stacked if c == chunks - 1 else along_y(stacked, w_ref)
+        mixed_high, mixed_low = split_pair(mixed)
         for m in range(low, high):
             for z in range(depth):
                 at = ((m - low) * depth + z) * tall

time: 26.6 us -> 26.5 us (level)
  no operation moved by 1% of the time
where the time goes in v6:
time: 26.5 us; the launch traced here: 26.3 us
  Pallas kernels  24.8 us (94%)
  local copies, waits for them, and re-layouts  0.84 us (3%)
  between operations  0.66 us (2%)
    pallas_call x1, Pallas kernels, body(): pl.pallas_call(functools.partial(kernel, dims), out_shape=pltpu.VMEM((1,...  24.8 us
    unnamed x1, local copies, waits for them, and re-layouts  0.84 us

profile of v6, /device:TPU:17, one launch (start us, length us, event | category | flops | bytes accessed | tf_op | source)
XLA Modules:
  0.0 26.3 jit_solution(15850162937432586650)
XLA Ops:
  0.7 24.8 %shard_map.73 = f32[1,5,2,128,128]{4,3,2,1,0:T(8,128)S(1)} custom-call(f32[1]{0:T(128)S(6)} %copy.10.step_ref, f32[2,128,128]{2,1,0:T(8,128)} %initial_hbm.1, f32[1,2,128,128]{3,2,1,0:T(8,128)} %guess_hbm.1, f32[1,5,2,128,128]{4,3,2,1,0:T(8,128)} %forcing_hbm.1, bf16[128,256]{1,0:T(8,128)(2,1)} %constant.15.x_hbm, bf16[128,128]{1,0:T(8,128)(2,1)} %constant.18.low_hbm, ...), custom_call_target="tpu_custom_call" | custom-call | tf_op jit(solution)/shard_map/pallas_call | solution.py:757
  25.5 0.8 %copy.9 = f32[1,5,2,128,128]{4,3,2,1,0:T(8,128)} copy(f32[1,5,2,128,128]{4,3,2,1,0:T(8,128)S(1)} %shard_map.73) | data formatting | bytes 1310720

commit v7 on v6

--- a/solution.py
+++ b/solution.py
@@ -384,7 +384,7 @@
                     pl.when(family == last_group)(lambda: pl.semaphore_wait(barrier, group - 1))
                     tell(open_sem)
 
-    halves = ((0, 3), (3, 5))
+    halves = ((0, 4), (4, 5))
 
     def o_groups(c):
         return halves if c == chunks - 1 else ((0, 5),)
@@ -665,7 +665,7 @@
             for c in range(max(0, chunks - lag), chunks):
                 give_later(c)
 
-        soon = jnp.logical_and(family > 0, mine < group // 2)
+        soon = jnp.logical_and(family > 0, mine < group - 1)
         pl.when(soon)(lambda: later(1))
         pl.when(jnp.logical_and(place > 0, jnp.logical_not(soon)))(lambda: later(2))
 

time: 26.5 us -> 26.6 us (level)
  no operation moved by 1% of the time
where the time goes in v7:
time: 26.6 us; the launch traced here: 26.4 us
  Pallas kernels  24.9 us (94%)
  local copies, waits for them, and re-layouts  0.84 us (3%)
  between operations  0.66 us (2%)
    pallas_call x1, Pallas kernels, body(): pl.pallas_call(functools.partial(kernel, dims), out_shape=pltpu.VMEM((1,...  24.9 us
    unnamed x1, local copies, waits for them, and re-layouts  0.84 us

profile of v7, /device:TPU:17, one launch (start us, length us, event | category | flops | bytes accessed | tf_op | source)
XLA Modules:
  0.0 26.4 jit_solution(306102226784637590)
XLA Ops:
  0.7 24.9 %shard_map.73 = f32[1,5,2,128,128]{4,3,2,1,0:T(8,128)S(1)} custom-call(f32[1]{0:T(128)S(6)} %copy.10.step_ref, f32[2,128,128]{2,1,0:T(8,128)} %initial_hbm.1, f32[1,2,128,128]{3,2,1,0:T(8,128)} %guess_hbm.1, f32[1,5,2,128,128]{4,3,2,1,0:T(8,128)} %forcing_hbm.1, bf16[128,256]{1,0:T(8,128)(2,1)} %constant.15.x_hbm, bf16[128,128]{1,0:T(8,128)(2,1)} %constant.18.low_hbm, ...), custom_call_target="tpu_custom_call" | custom-call | tf_op jit(solution)/shard_map/pallas_call | solution.py:757
  25.6 0.8 %copy.9 = f32[1,5,2,128,128]{4,3,2,1,0:T(8,128)} copy(f32[1,5,2,128,128]{4,3,2,1,0:T(8,128)S(1)} %shard_map.73) | data formatting | bytes 1310720
